TPU v7x, 256 devices: a whole 4x4x8 slice. The times are simulated.
256 devices in a mesh: seq: 16 (over z, core), dp: 16 (over x, y).
Axes of the slice: x: 4, y: 4, z: 8, core: 2. Of those that a mesh axis runs over, the one named last changes fastest.
Arguments:
- raw_query: bfloat16 [16, 4096, 2048], P('dp', 'seq'), may hold values from -4 to 4
- raw_key: bfloat16 [16, 4096, 2048], P('dp', 'seq'), may hold values from -4 to 4
- raw_value: bfloat16 [16, 4096, 2048], P('dp', 'seq'), may hold values from -6 to 6
- query_gain: float32 [128], replicated, may hold values from 0.5 to 8
- key_gain: float32 [128], replicated, may hold values from 0.5 to 8
- lengths: int32 [64], replicated, may hold values from 1 to 4096, 65536 in all
- clip_grids: int32 [64, 2], replicated, may hold values from 4 to 23
Outputs:
- attended: bfloat16 [16, 4096, 2048], P('dp', 'seq')
All inputs are finite; a program needn't handle non-finite values.
Results may differ from a plain program's by a relative error of at most 0.0017.
The roundings to bfloat16 on the way count: a program that leaves them out, or rounds other values in their place, can miss the bound.
Values may be sent and summed in bfloat16 or wider, within the bound.
No kernel may reach another device: no remote copies, remote signals or barrier semaphores. Data moves between devices by JAX's collectives and lax.ppermute only.
A program may use at most 64 MiB of HBM per device.

v0:
```python
import functools
import math

import jax
import jax.numpy as jnp
import numpy as np
from jax import lax
from jax.experimental import pallas as pl
from jax.experimental.pallas import tpu as pltpu
from jax.sharding import Mesh
from jax.sharding import PartitionSpec as P


NORM_EPS = 1e-06
ROPE_THETA = 256.0
SCORE_SCALE = 1.0 / math.sqrt(128.0)
MASK_FLOOR = -1e30
EXP2_SCALE = SCORE_SCALE * math.log2(math.e)
TILE = 512
SUB = 256
GROUPS = ((0, 2), (4, 3), (5, 6), (7, 1))
ARRIVAL = (1, 7, 2, 6, 3, 5, 4)
PIECES = ((1, 7), (2, 6), (3, 5), (0, 4))
BF16 = jnp.bfloat16
HBM = pl.BlockSpec(memory_space=pltpu.HBM)
VMEM = pl.BlockSpec(memory_space=pltpu.VMEM)
SMEM = pl.BlockSpec(memory_space=pltpu.SMEM)


def rate_rows():
    pair = np.arange(128) // 2
    real = pair.astype(np.float64)
    time_rate = np.where(pair < 8, ROPE_THETA ** (-2.0 * real / 16.0), 0.0)
    height_rate = np.where(
        (pair >= 8) & (pair < 36), ROPE_THETA ** (-2.0 * (real - 8.0) / 56.0), 0.0
    )
    width_rate = np.where(pair >= 36, ROPE_THETA ** (-2.0 * (real - 36.0) / 56.0), 0.0)
    return tuple(jnp.asarray(r, jnp.float32) for r in (time_rate, height_rate, width_rate))


def rope_tables(rows, starts, ends, clip_grids):
    inside = ((rows[:, None] >= starts[None, :]) & (rows[:, None] < ends[None, :])).astype(
        jnp.int32
    )
    clip_start = jnp.sum(inside * starts[None, :], axis=1)
    height = jnp.sum(inside * clip_grids[None, :, 0], axis=1)
    breadth = jnp.sum(inside * clip_grids[None, :, 1], axis=1)
    offset = rows - clip_start
    frame = offset // (height * breadth)
    row = offset // breadth % height
    col = offset % breadth
    time_rate, height_rate, width_rate = rate_rows()
    angles = (
        frame.astype(jnp.float32)[:, None] * time_rate[None, :]
        + row.astype(jnp.float32)[:, None] * height_rate[None, :]
        + col.astype(jnp.float32)[:, None] * width_rate[None, :]
    )
    return jnp.cos(angles), jnp.sin(angles)


def rotate(x, even, gain, cos, sin):
    x = x.astype(jnp.float32)
    mean = jnp.mean(x * x, axis=-1, keepdims=True)
    x = x * lax.rsqrt(mean + NORM_EPS) * gain
    swapped = jnp.where(even, -pltpu.roll(x, 127, 1), pltpu.roll(x, 1, 1))
    return (x * cos + swapped * sin).astype(BF16)


def even_lanes():
    return lax.rem(lax.broadcasted_iota(jnp.int32, (SUB, 128), 1), 2) == 0


def key_value_body(pos, key, value, gain, cos, sin, keep, send):
    even = even_lanes()

    def one(k, carry):
        head = 2 * lax.rem(pos[0] + k, 8)
        for slot, out in ((pos[1], keep), (1 - pos[1], send)):
            column = pl.ds(pl.multiple_of((head + slot) * 128, 128), 128)
            out[k, 0] = rotate(key[:, column], even, gain[...], cos[...], sin[...])
            out[k, 1, 0:128] = value[0:128, column].T
            out[k, 1, 128:256] = value[128:256, column].T
        return carry

    lax.fori_loop(0, 8, one, 0)


def query_body(pos, query, gain, cos, sin, keep, send):
    even = even_lanes()

    def one(k, carry):
        head = 2 * lax.rem(pos[0] + k, 8)
        for slot, out in ((pos[1], keep), (1 - pos[1], send)):
            column = pl.ds(pl.multiple_of((head + slot) * 128, 128), 128)
            out[k] = rotate(query[:, column], even, gain[...], cos[...], sin[...])
        return carry

    lax.fori_loop(0, 8, one, 0)


def head_blocks(body, dims, *args):
    out = jax.ShapeDtypeStruct((8,) + dims, BF16)
    return pl.pallas_call(
        body,
        out_shape=(out, out),
        in_specs=[SMEM] + [VMEM] * (len(args) - 1),
        out_specs=(VMEM, VMEM),
        cost_estimate=pl.CostEstimate(
            flops=2_000_000_000, transcendentals=8192, bytes_accessed=4_000_000
        ),
    )(*args)


def attend_body(sc, q0, q1, qse, *refs):
    kv, (o0, o1), scratch = refs[:12], refs[12:14], refs[14:]
    buf, sem, flag, qbuf, acc, s0, s1, p0, p1 = scratch
    zpos, core = sc[0], sc[1]
    scores, probs = (s0, s1), (p0, p1)
    low_all = sc[2] // TILE
    high_all = (sc[5] + TILE - 1) // TILE
    for i in range(1, 4):
        low_all = jnp.minimum(low_all, sc[2 + 4 * i] // TILE)
        high_all = jnp.maximum(high_all, (sc[5 + 4 * i] + TILE - 1) // TILE)

    def start(t, carry):
        pack = t // 8
        rel = lax.rem(t - pack * 8 - zpos + 8, 8)
        piece = lax.rem(jnp.minimum(rel, 8 - rel) + 3, 4)
        for n in range(12):

            @pl.when(pack * 4 + piece == n)
            def _():
                pltpu.make_async_copy(kv[n].at[rel // 4], buf.at[t], sem.at[t]).start()

        flag[t] = 0
        return carry

    lax.fori_loop(low_all, high_all, start, 0)

    def ensure(t):
        @pl.when(flag[t] == 0)
        def _():
            pltpu.make_async_copy(kv[0].at[0], buf.at[t], sem.at[t]).wait()
            flag[t] = 1

    qbuf[0:2] = q0[...]
    qbuf[2:4] = q1[...]

    def one(i, carry):
        base = 2 + 4 * i
        low = sc[base] // TILE
        high = (sc[base + 3] + TILE - 1) // TILE
        last_start, first_end = sc[base + 1], sc[base + 2]

        def score(t, into):
            for j in range(2):
                into[pl.ds(SUB * j, SUB), :] = lax.dot_general(
                    buf[t, j, 0],
                    qbuf[i],
                    (((1,), (1,)), ((), ())),
                    preferred_element_type=jnp.float32,
                )

        def weigh(t, source):
            parts = []
            for j in range(2):
                turned = jnp.concatenate([buf[t, j, 1, 0:128], buf[t, j, 1, 128:256]], axis=1)
                rows = source[SUB * j : SUB * j + SUB, :]
                parts.append(jnp.dot(turned, rows, preferred_element_type=jnp.float32))
            return parts[0] + parts[1]

        def step(parity, masked, t, carry):
            top, total, shrink = carry
            score(jnp.minimum(t + 1, high - 1), scores[1 - parity])
            acc[...] = acc[...] * shrink + weigh(jnp.maximum(t - 1, low), probs[1 - parity])
            s = scores[parity][...]
            if masked:
                row = lax.broadcasted_iota(jnp.int32, (TILE, SUB), 0)
                key = (row ^ (core * SUB)) + t * TILE
                s = jnp.where((key >= qse[i, 0:1, :]) & (key < qse[i, 1:2, :]), s, MASK_FLOOR)
            new_top = jnp.maximum(top, jnp.max(s, axis=0, keepdims=True))
            shrink = jnp.exp2((top - new_top) * EXP2_SCALE)
            p = jnp.exp2((s - new_top) * EXP2_SCALE)
            total = total * shrink + jnp.sum(p, axis=0, keepdims=True)
            probs[parity][...] = p.astype(BF16)
            return new_top, total, shrink

        ensure(low)
        score(low, s0)
        acc[...] = jnp.zeros_like(acc)
        p1[...] = jnp.zeros_like(p1)

        def loop(t, carry):
            @pl.when(t + 1 < high)
            def _():
                ensure(t + 1)

            full = (last_start <= t * TILE) & (t * TILE + TILE <= first_end)
            which = lax.rem(t - low, 2) * 2 + jnp.where(full, 0, 1)
            kinds = [
                functools.partial(step, parity, masked, t)
                for parity in (0, 1)
                for masked in (False, True)
            ]
            return lax.switch(which, kinds, carry)

        first = (
            jnp.full((1, SUB), MASK_FLOOR, jnp.float32),
            jnp.zeros((1, SUB), jnp.float32),
            jnp.ones((1, SUB), jnp.float32),
        )
        _, total, shrink = lax.fori_loop(low, high, loop, first)

        def finish(source):
            out = ((acc[...] * shrink + weigh(high - 1, source)) / total).T.astype(BF16)

            @pl.when(i < 2)
            def _():
                o0[jnp.minimum(i, 1)] = out

            @pl.when(i >= 2)
            def _():
                o1[jnp.maximum(i - 2, 0)] = out

        last = lax.rem(high - 1 - low, 2)
        pl.when(last == 0)(lambda: finish(p0))
        pl.when(last == 1)(lambda: finish(p1))
        return carry

    lax.fori_loop(0, 4, one, 0)

    def drain(t, carry):
        ensure(t)
        return carry

    lax.fori_loop(low_all, high_all, drain, 0)


def attend(sc, q0, q1, qse, blocks):
    block = jax.ShapeDtypeStruct((2, SUB, 128), BF16)
    return pl.pallas_call(
        attend_body,
        out_shape=(block, block),
        in_specs=[SMEM, VMEM, VMEM, VMEM] + [HBM] * 12,
        out_specs=(VMEM, VMEM),
        scratch_shapes=[
            pltpu.VMEM((24, 2, 2, SUB, 128), BF16),
            pltpu.SemaphoreType.DMA((24,)),
            pltpu.SMEM((24,), jnp.int32),
            pltpu.VMEM((4, SUB, 128), BF16),
            pltpu.VMEM((128, SUB), jnp.float32),
            pltpu.VMEM((TILE, SUB), jnp.float32),
            pltpu.VMEM((TILE, SUB), jnp.float32),
            pltpu.VMEM((TILE, SUB), BF16),
            pltpu.VMEM((TILE, SUB), BF16),
        ],
        compiler_params=pltpu.CompilerParams(vmem_limit_bytes=40 << 20),
        cost_estimate=pl.CostEstimate(
            flops=12_000_000_000, transcendentals=4_000_000, bytes_accessed=8_000_000
        ),
    )(sc, q0, q1, qse, *blocks)


def place_body(pos, *refs):
    mine, swapped_a, swapped_b, out = refs[:8], refs[8], refs[9], refs[10]
    for n, rel in enumerate(RETURN_ORDER):
        head = 2 * lax.rem(pos[0] + rel, 8)
        other = swapped_a[n] if n < 6 else swapped_b[n - 6]
        for block, slot in ((mine[n][0], pos[1]), (other, 1 - pos[1])):
            out[:, pl.ds(pl.multiple_of((head + slot) * 128, 128), 128)] = block


RETURN_ORDER = tuple((8 - rel) % 8 for group in GROUPS for rel in group)


def place(pos, mine, swapped_a, swapped_b):
    return pl.pallas_call(
        place_body,
        out_shape=jax.ShapeDtypeStruct((SUB, 2048), BF16),
        in_specs=[SMEM] + [VMEM] * 10,
        out_specs=VMEM,
    )(pos, *mine, swapped_a, swapped_b)


def core_swap(x):
    return lax.ppermute(x, "c", [(0, 1), (1, 0)])


def z_shift(x, k):
    return lax.ppermute(x, "z", [(i, (i + k) % 8) for i in range(8)])


def gather_heads(keep, send, order):
    other = core_swap(send)
    arrived = {0: jnp.stack([keep[0], other[0]])}
    for rel in order:
        k = (8 - rel) % 8
        block = jnp.stack([keep[k], other[k]])
        arrived[rel] = z_shift(block, k)
    return arrived


def with_neighbours(arrived):
    forward = [(i, i + 1) for i in range(15)]
    backward = [(i + 1, i) for i in range(15)]
    pieces = [jnp.stack([arrived[a], arrived[b]]) for a, b in PIECES]
    before, after = [], []
    for piece in pieces:
        before.append(lax.ppermute(piece, "dp", forward))
        after.append(lax.ppermute(piece, "dp", backward))
    return before + pieces + after


def compute(raw_query, raw_key, raw_value, query_gain, key_gain, lengths, clip_grids):
    zpos, core, dpos = lax.axis_index("z"), lax.axis_index("c"), lax.axis_index("dp")
    pos = jnp.stack([zpos, core]).astype(jnp.int32)
    query, key, value = raw_query[0], raw_key[0], raw_value[0]
    ends = jnp.cumsum(lengths).astype(jnp.int32)
    starts = ends - lengths
    pack_base = dpos * 4096
    rows = pack_base + zpos * 512 + core * 256 + jnp.arange(SUB, dtype=jnp.int32)

    cos, sin = rope_tables(rows, starts, ends, clip_grids)
    blocks = with_neighbours(
        gather_heads(
            *head_blocks(
                key_value_body, (2, SUB, 128), pos, key, value, key_gain.reshape(1, 128), cos, sin
            ),
            ARRIVAL,
        )
    )
    order = [rel for group in GROUPS for rel in group]
    query_blocks = head_blocks(
        query_body, (SUB, 128), pos, query, query_gain.reshape(1, 128), cos, sin
    )
    queries = gather_heads(*query_blocks, order[1:])

    rels = np.array(order, np.int32)
    chip = (zpos + rels) % 8
    side = jnp.stack([core, 1 - core])
    first = pack_base + chip[:, None] * 512 + side[None, :] * 256
    tokens = (first[:, :, None] + jnp.arange(SUB, dtype=jnp.int32)).reshape(16 * SUB)
    base = pack_base - 4096
    began = jnp.max(jnp.where(tokens[:, None] >= starts[None, :], starts[None, :], 0), axis=1)
    ended = jnp.min(jnp.where(tokens[:, None] < ends[None, :], ends[None, :], 65536), axis=1)
    qse = jnp.stack([(began - base).reshape(16, SUB), (ended - base).reshape(16, SUB)], axis=1)
    bounds = qse[:, :, :: SUB - 1].reshape(16, 4)

    returned = []
    for n, (a, b) in enumerate(GROUPS):
        sc = jnp.concatenate([pos, bounds[4 * n : 4 * n + 4].reshape(16)])
        outs = attend(sc, queries[a], queries[b], qse[4 * n : 4 * n + 4], blocks)
        for rel, out in zip((a, b), outs):
            returned.append(z_shift(out, rel) if rel else out)
    swapped_a = core_swap(jnp.stack([r[1] for r in returned[:6]]))
    swapped_b = core_swap(jnp.stack([r[1] for r in returned[6:]]))
    return place(pos, returned, swapped_a, swapped_b).reshape(1, SUB, 2048)


def solution(mesh):
    split = Mesh(mesh.devices.reshape(8, 2, mesh.shape["dp"]), ("z", "c", "dp"))
    token = P("dp", ("z", "c"), None)
    return jax.shard_map(
        compute,
        mesh=split,
        in_specs=(token, token, token, P(), P(), P(), P()),
        out_specs=token,
        check_vma=False,
    )
```

profile of v0, /device:TPU:5, one launch (start us, length us, event | category | flops | bytes accessed | tf_op | source)
XLA Modules:
  0.0 236.9 jit_solution(17027483157567001877)
XLA Ops:
  0.0 0.7 copy-done.12
  0.7 0.7 copy-done.13
  3.3 1.3 fusion
  4.6 5.4 %shard_map.109 = (bf16[8,256,128]{2,1,0:T(8,128)(2,1)}, bf16[8,256,128]{2,1,0:T(8,128)(2,1)}) custom-call(s32[2]{0:T(128)} %get-tuple-element.86.pos, bf16[256,2048]{1,0:T(8,128)(2,1)} %bitcast.41, f32[1,128]{1,0:T(1,128)} %bitcast.44, f32[256,128]{1,0:T(8,128)} %get-tuple-element.77.cos, f32[256,128]{1,0:T(8,128)} %get-tuple-element.76.sin), custom_call_target="tpu_custom_call" | custom-call | flops 2000000000 | bytes 4000000 | tf_op jit(solution)/shard_map/pallas_call | solution.py:103
  10.0 0.7 collective-permute-start
  10.6 6.4 %shard_map.110 = (bf16[8,2,256,128]{3,2,1,0:T(8,128)(2,1)}, bf16[8,2,256,128]{3,2,1,0:T(8,128)(2,1)}) custom-call(s32[2]{0:T(128)} %get-tuple-element.86.pos, bf16[256,2048]{1,0:T(8,128)(2,1)} %bitcast.42, bf16[256,2048]{1,0:T(8,128)(2,1)} %bitcast.43, f32[1,128]{1,0:T(1,128)} %bitcast.45, f32[256,128]{1,0:T(8,128)} %get-tuple-element.77.cos, ...), custom_call_target="tpu_custom_call" | custom-call | flops 2000000000 | bytes 4000000 | tf_op jit(solution)/shard_map/pallas_call | solution.py:103
  18.6 1.3 collective-permute-done.2
  20.1 5.7 %collective-permute-start.3 = (bf16[2,2,256,128]{3,2,1,0:T(8,128)(2,1)S(1)}, bf16[2,2,256,128]{3,2,1,0:T(8,128)(2,1)S(1)}, u32[]{:S(2)}, u32[]{:S(2)}) collective-permute-start(bf16[2,2,256,128]{3,2,1,0:T(8,128)(2,1)S(1)} %pad_maximum_fusion.4), channel_id=1, source_target_pairs={{0,224},{32,0},{64,32},{96,64},{128,96},{160,128},{192,160},{224,1... | collective-permute-start | bytes 786440 | tf_op jit(solution)/shard_map/ppermute | solution.py:290
  25.9 2.4 %collective-permute-start.9 = (bf16[2,2,256,128]{3,2,1,0:T(8,128)(2,1)S(1)}, bf16[2,2,256,128]{3,2,1,0:T(8,128)(2,1)S(1)}, u32[]{:S(2)}, u32[]{:S(2)}) collective-permute-start(bf16[2,2,256,128]{3,2,1,0:T(8,128)(2,1)S(1)} %pad_maximum_fusion.8), channel_id=1, source_target_pairs={{0,160},{32,192},{64,224},{96,0},{128,32},{160,64},{192,96},{224,1... | collective-permute-start | bytes 786440 | tf_op jit(solution)/shard_map/ppermute | solution.py:290
  28.3 1.0 collective-permute-start.10
  29.3 2.9 %collective-permute-start.12 = (bf16[2,2,256,128]{3,2,1,0:T(8,128)(2,1)S(1)}, bf16[2,2,256,128]{3,2,1,0:T(8,128)(2,1)S(1)}, u32[]{:S(2)}, u32[]{:S(2)}) collective-permute-start(bf16[2,2,256,128]{3,2,1,0:T(8,128)(2,1)S(1)} %pad_maximum_fusion.10), channel_id=1, source_target_pairs={{0,128},{32,160},{64,192},{96,224},{128,0},{160,32},{192,64},{224,... | collective-permute-start | bytes 786440 | tf_op jit(solution)/shard_map/ppermute | solution.py:290
  32.3 24.2 %collective-permute-done.12 = bf16[2,2,256,128]{3,2,1,0:T(8,128)(2,1)S(1)} collective-permute-done((bf16[2,2,256,128]{3,2,1,0:T(8,128)(2,1)S(1)}, bf16[2,2,256,128]{3,2,1,0:T(8,128)(2,1)S(1)}, u32[]{:S(2)}, u32[]{:S(2)}) %collective-permute-start.12) | collective-permute-done | bytes 262176 | tf_op jit(solution)/shard_map/ppermute | solution.py:290
  56.5 6.3 %collective-permute-start.6 = (bf16[2,2,256,128]{3,2,1,0:T(8,128)(2,1)S(1)}, bf16[2,2,256,128]{3,2,1,0:T(8,128)(2,1)S(1)}, u32[]{:S(2)}, u32[]{:S(2)}) collective-permute-start(bf16[2,2,256,128]{3,2,1,0:T(8,128)(2,1)S(1)} %pad_maximum_fusion.6), channel_id=1, source_target_pairs={{0,192},{32,224},{64,0},{96,32},{128,64},{160,96},{192,128},{224,1... | collective-permute-start | bytes 786440 | tf_op jit(solution)/shard_map/ppermute | solution.py:290
  62.8 1.2 collective-permute-start.7
  64.0 4.6 %collective-permute-start.17 = (bf16[2,2,2,256,128]{4,3,2,1,0:T(8,128)(2,1)S(1)}, bf16[2,2,2,256,128]{4,3,2,1,0:T(8,128)(2,1)S(1)}, u32[]{:S(2)}, u32[]{:S(2)}) collective-permute-start(bf16[2,2,2,256,128]{4,3,2,1,0:T(8,128)(2,1)S(1)} %pad_maximum_fusion.3.refs_7_), channel_id=1, source_target_pairs={{1,0},{2,1},{3,2},{4,3},{5,4},{6,5},{7,6},{8,7},{9,8},{10,9},{11,1... | collective-permute-start | bytes 1572872 | tf_op jit(solution)/shard_map/ppermute | solution.py:310
  68.7 1.9 collective-permute-start.13
  70.6 5.5 %collective-permute-start.16 = (bf16[2,2,2,256,128]{4,3,2,1,0:T(8,128)(2,1)S(1)}, bf16[2,2,2,256,128]{4,3,2,1,0:T(8,128)(2,1)S(1)}, u32[]{:S(2)}, u32[]{:S(2)}) collective-permute-start(bf16[2,2,2,256,128]{4,3,2,1,0:T(8,128)(2,1)S(1)} %pad_maximum_fusion.2.refs_6_), channel_id=1, source_target_pairs={{1,0},{2,1},{3,2},{4,3},{5,4},{6,5},{7,6},{8,7},{9,8},{10,9},{11,1... | collective-permute-start | bytes 1572872 | tf_op jit(solution)/shard_map/ppermute | solution.py:310
  76.2 1.8 collective-permute-start.23
  78.0 2.0 collective-permute-start.24
  80.1 7.1 %collective-permute-done.23.q0 = bf16[2,256,128]{2,1,0:T(8,128)(2,1)S(1)} collective-permute-done((bf16[2,256,128]{2,1,0:T(8,128)(2,1)S(1)}, bf16[2,256,128]{2,1,0:T(8,128)(2,1)S(1)}, u32[]{:S(2)}, u32[]{:S(2)}) %collective-permute-start.23) | collective-permute-done | bytes 131104 | tf_op jit(solution)/shard_map/ppermute | solution.py:290
  87.2 2.9 %collective-permute-start.11 = (bf16[2,2,2,256,128]{4,3,2,1,0:T(8,128)(2,1)S(1)}, bf16[2,2,2,256,128]{4,3,2,1,0:T(8,128)(2,1)S(1)}, u32[]{:S(2)}, u32[]{:S(2)}) collective-permute-start(bf16[2,2,2,256,128]{4,3,2,1,0:T(8,128)(2,1)S(1)} %pad_maximum_fusion.2.refs_6_), channel_id=1, source_target_pairs={{0,1},{1,2},{2,3},{3,4},{4,5},{5,6},{6,7},{7,8},{8,9},{9,10},{10,1... | collective-permute-start | bytes 1572872 | tf_op jit(solution)/shard_map/ppermute | solution.py:309
  90.0 4.3 %collective-permute-done.24.q1 = bf16[2,256,128]{2,1,0:T(8,128)(2,1)S(1)} collective-permute-done((bf16[2,256,128]{2,1,0:T(8,128)(2,1)S(1)}, bf16[2,256,128]{2,1,0:T(8,128)(2,1)S(1)}, u32[]{:S(2)}, u32[]{:S(2)}) %collective-permute-start.24) | collective-permute-done | bytes 131104 | tf_op jit(solution)/shard_map/ppermute | solution.py:290
  94.3 4.0 %collective-permute-start.15 = (bf16[2,2,2,256,128]{4,3,2,1,0:T(8,128)(2,1)S(1)}, bf16[2,2,2,256,128]{4,3,2,1,0:T(8,128)(2,1)S(1)}, u32[]{:S(2)}, u32[]{:S(2)}) collective-permute-start(bf16[2,2,2,256,128]{4,3,2,1,0:T(8,128)(2,1)S(1)} %pad_maximum_fusion.1.refs_5_), channel_id=1, source_target_pairs={{1,0},{2,1},{3,2},{4,3},{5,4},{6,5},{7,6},{8,7},{9,8},{10,9},{11,1... | collective-permute-start | bytes 1572872 | tf_op jit(solution)/shard_map/ppermute | solution.py:310
  98.3 1.9 collective-permute-start.8
  100.2 5.5 %collective-permute-start.14 = (bf16[2,2,2,256,128]{4,3,2,1,0:T(8,128)(2,1)S(1)}, bf16[2,2,2,256,128]{4,3,2,1,0:T(8,128)(2,1)S(1)}, u32[]{:S(2)}, u32[]{:S(2)}) collective-permute-start(bf16[2,2,2,256,128]{4,3,2,1,0:T(8,128)(2,1)S(1)} %pad_maximum_fusion.refs_4_), channel_id=1, source_target_pairs={{1,0},{2,1},{3,2},{4,3},{5,4},{6,5},{7,6},{8,7},{9,8},{10,9},{11,1... | collective-permute-start | bytes 1572872 | tf_op jit(solution)/shard_map/ppermute | solution.py:310
  105.7 2.1 collective-permute-start.5
  108.1 6.6 %collective-permute-start.19 = (bf16[2,256,128]{2,1,0:T(8,128)(2,1)S(1)}, bf16[2,256,128]{2,1,0:T(8,128)(2,1)S(1)}, u32[]{:S(2)}, u32[]{:S(2)}) collective-permute-start(bf16[2,256,128]{2,1,0:T(8,128)(2,1)S(1)} %pad_maximum_fusion.13), channel_id=1, source_target_pairs={{0,128},{32,160},{64,192},{96,224},{128,0},{160,32},{192,64},{224,... | collective-permute-start | bytes 393224 | tf_op jit(solution)/shard_map/ppermute | solution.py:290
  114.7 3.9 %collective-permute-start.20 = (bf16[2,256,128]{2,1,0:T(8,128)(2,1)S(1)}, bf16[2,256,128]{2,1,0:T(8,128)(2,1)S(1)}, u32[]{:S(2)}, u32[]{:S(2)}) collective-permute-start(bf16[2,256,128]{2,1,0:T(8,128)(2,1)S(1)} %pad_maximum_fusion.14), channel_id=1, source_target_pairs={{0,160},{32,192},{64,224},{96,0},{128,32},{160,64},{192,96},{224,1... | collective-permute-start | bytes 393224 | tf_op jit(solution)/shard_map/ppermute | solution.py:290
  118.9 5.1 %collective-permute-start.27 = (bf16[2,256,128]{2,1,0:T(8,128)(2,1)S(1)}, bf16[2,256,128]{2,1,0:T(8,128)(2,1)S(1)}, u32[]{:S(2)}, u32[]{:S(2)}) collective-permute-start(bf16[2,256,128]{2,1,0:T(8,128)(2,1)S(1)} %pad_maximum_fusion.17), channel_id=1, source_target_pairs={{0,32},{32,64},{64,96},{96,128},{128,160},{160,192},{192,224},{224... | collective-permute-start | bytes 393224 | tf_op jit(solution)/shard_map/ppermute | solution.py:290
  124.0 1.3 collective-permute-done.5.refs_0_
  125.3 3.3 %collective-permute-start.28 = (bf16[2,256,128]{2,1,0:T(8,128)(2,1)S(1)}, bf16[2,256,128]{2,1,0:T(8,128)(2,1)S(1)}, u32[]{:S(2)}, u32[]{:S(2)}) collective-permute-start(bf16[2,256,128]{2,1,0:T(8,128)(2,1)S(1)} %pad_maximum_fusion.18), channel_id=1, source_target_pairs={{0,224},{32,0},{64,32},{96,64},{128,96},{160,128},{192,160},{224,1... | collective-permute-start | bytes 393224 | tf_op jit(solution)/shard_map/ppermute | solution.py:290
  128.6 12.3 %shard_map.113 = (bf16[2,256,128]{2,1,0:T(8,128)(2,1)S(1)}, bf16[2,256,128]{2,1,0:T(8,128)(2,1)S(1)}) custom-call(s32[18]{0:T(128)S(1)} %get-tuple-element.83.sc, bf16[2,256,128]{2,1,0:T(8,128)(2,1)S(1)} %collective-permute-done.23.q0, bf16[2,256,128]{2,1,0:T(8,128)(2,1)S(1)} %collective-permute-done.24.q1, s32[4,2,256]{2,1,0:T(2,128)S(1)} %get-tuple-element.71.qse, ...), custom_call_target="tpu_custom_call" | custom-call | flops 12000000000 | bytes 8000000 | tf_op jit(solution)/shard_map/pallas_call | solution.py:241
  140.9 1.5 collective-permute-start.25
  142.4 14.4 %shard_map.111 = (bf16[2,256,128]{2,1,0:T(8,128)(2,1)S(1)}, bf16[2,256,128]{2,1,0:T(8,128)(2,1)S(1)}) custom-call(s32[18]{0:T(128)S(1)} %get-tuple-element.85.sc, bf16[2,256,128]{2,1,0:T(8,128)(2,1)S(1)} %pad_maximum_fusion.11.q0, bf16[2,256,128]{2,1,0:T(8,128)(2,1)S(1)} %collective-permute-done.1.q1, s32[4,2,256]{2,1,0:T(2,128)S(1)} %get-tuple-element.69.qse, ...), custom_call_target="tpu_custom_call" | custom-call | flops 12000000000 | bytes 8000000 | tf_op jit(solution)/shard_map/pallas_call | solution.py:241
  156.8 11.2 %collective-permute-start.26 = (bf16[2,256,128]{2,1,0:T(8,128)(2,1)S(1)}, bf16[2,256,128]{2,1,0:T(8,128)(2,1)S(1)}, u32[]{:S(2)}, u32[]{:S(2)}) collective-permute-start(bf16[2,256,128]{2,1,0:T(8,128)(2,1)S(1)} %get-tuple-element.26), channel_id=1, source_target_pairs={{0,192},{32,224},{64,0},{96,32},{128,64},{160,96},{192,128},{224,1... | collective-permute-start | bytes 393224 | tf_op jit(solution)/shard_map/ppermute | solution.py:290
  167.9 9.7 %shard_map.112 = (bf16[2,256,128]{2,1,0:T(8,128)(2,1)S(1)}, bf16[2,256,128]{2,1,0:T(8,128)(2,1)S(1)}) custom-call(s32[18]{0:T(128)S(1)} %get-tuple-element.84.sc, bf16[2,256,128]{2,1,0:T(8,128)(2,1)S(1)} %collective-permute-done.19.q0, bf16[2,256,128]{2,1,0:T(8,128)(2,1)S(1)} %collective-permute-done.20.q1, s32[4,2,256]{2,1,0:T(2,128)S(1)} %get-tuple-element.70.qse, ...), custom_call_target="tpu_custom_call" | custom-call | flops 12000000000 | bytes 8000000 | tf_op jit(solution)/shard_map/pallas_call | solution.py:241
  177.7 8.7 %collective-permute-start.21 = (bf16[2,256,128]{2,1,0:T(8,128)(2,1)S(1)}, bf16[2,256,128]{2,1,0:T(8,128)(2,1)S(1)}, u32[]{:S(2)}, u32[]{:S(2)}) collective-permute-start(bf16[2,256,128]{2,1,0:T(8,128)(2,1)S(1)} %get-tuple-element.23), channel_id=1, source_target_pairs={{0,128},{32,160},{64,192},{96,224},{128,0},{160,32},{192,64},{224,... | collective-permute-start | bytes 393224 | tf_op jit(solution)/shard_map/ppermute | solution.py:290
  186.4 2.4 %collective-permute-done.21.refs_2_ = bf16[2,256,128]{2,1,0:T(8,128)(2,1)S(1)} collective-permute-done((bf16[2,256,128]{2,1,0:T(8,128)(2,1)S(1)}, bf16[2,256,128]{2,1,0:T(8,128)(2,1)S(1)}, u32[]{:S(2)}, u32[]{:S(2)}) %collective-permute-start.21) | collective-permute-done | bytes 131104 | tf_op jit(solution)/shard_map/ppermute | solution.py:290
  188.9 7.7 %collective-permute-done.22.refs_3_ = bf16[2,256,128]{2,1,0:T(8,128)(2,1)S(1)} collective-permute-done((bf16[2,256,128]{2,1,0:T(8,128)(2,1)S(1)}, bf16[2,256,128]{2,1,0:T(8,128)(2,1)S(1)}, u32[]{:S(2)}, u32[]{:S(2)}) %collective-permute-start.22) | collective-permute-done | bytes 131104 | tf_op jit(solution)/shard_map/ppermute | solution.py:290
  197.2 7.1 %collective-permute-start.31 = (bf16[6,256,128]{2,1,0:T(8,128)(2,1)S(1)}, bf16[6,256,128]{2,1,0:T(8,128)(2,1)S(1)}, u32[]{:S(2)}, u32[]{:S(2)}) collective-permute-start(bf16[6,256,128]{2,1,0:T(8,128)(2,1)S(1)} %slice_dynamic-update-slice_fusion), channel_id=1, source_target_pairs={{0,16},{16,0},{1,17},{17,1},{2,18},{18,2},{3,19},{19,3},{4,20},{20... | collective-permute-start | bytes 1179656 | tf_op jit(solution)/shard_map/ppermute | solution.py:286
  204.3 15.9 %shard_map.114 = (bf16[2,256,128]{2,1,0:T(8,128)(2,1)S(1)}, bf16[2,256,128]{2,1,0:T(8,128)(2,1)S(1)}) custom-call(s32[18]{0:T(128)S(1)} %get-tuple-element.34.sc, bf16[2,256,128]{2,1,0:T(8,128)(2,1)S(1)} %collective-permute-done.27.q0, bf16[2,256,128]{2,1,0:T(8,128)(2,1)S(1)} %collective-permute-done.28.q1, s32[4,2,256]{2,1,0:T(2,128)S(1)} %get-tuple-element.68.qse, ...), custom_call_target="tpu_custom_call" | custom-call | flops 12000000000 | bytes 8000000 | tf_op jit(solution)/shard_map/pallas_call | solution.py:241
  220.2 3.8 %collective-permute-start.29 = (bf16[2,256,128]{2,1,0:T(8,128)(2,1)S(1)}, bf16[2,256,128]{2,1,0:T(8,128)(2,1)S(1)}, u32[]{:S(2)}, u32[]{:S(2)}) collective-permute-start(bf16[2,256,128]{2,1,0:T(8,128)(2,1)S(1)} %get-tuple-element.27), channel_id=1, source_target_pairs={{0,224},{32,0},{64,32},{96,64},{128,96},{160,128},{192,160},{224,1... | collective-permute-start | bytes 393224 | tf_op jit(solution)/shard_map/ppermute | solution.py:290
  224.0 2.8 %collective-permute-done.29.refs_6_ = bf16[2,256,128]{2,1,0:T(8,128)(2,1)S(1)} collective-permute-done((bf16[2,256,128]{2,1,0:T(8,128)(2,1)S(1)}, bf16[2,256,128]{2,1,0:T(8,128)(2,1)S(1)}, u32[]{:S(2)}, u32[]{:S(2)}) %collective-permute-start.29) | collective-permute-done | bytes 131104 | tf_op jit(solution)/shard_map/ppermute | solution.py:290
  226.9 3.1 %collective-permute-done.30.refs_7_ = bf16[2,256,128]{2,1,0:T(8,128)(2,1)S(1)} collective-permute-done((bf16[2,256,128]{2,1,0:T(8,128)(2,1)S(1)}, bf16[2,256,128]{2,1,0:T(8,128)(2,1)S(1)}, u32[]{:S(2)}, u32[]{:S(2)}) %collective-permute-start.30) | collective-permute-done | bytes 131104 | tf_op jit(solution)/shard_map/ppermute | solution.py:290
  230.6 1.2 collective-permute-start.32
  231.8 1.0 collective-permute-done.32.refs_9_
  233.4 0.7 copy-done.3
  234.2 2.7 %shard_map.115 = bf16[256,2048]{1,0:T(8,128)(2,1)} custom-call(s32[2]{0:T(128)} %get-tuple-element.86.pos, bf16[2,256,128]{2,1,0:T(8,128)(2,1)} %copy-done, bf16[2,256,128]{2,1,0:T(8,128)(2,1)} %copy-done.6, bf16[2,256,128]{2,1,0:T(8,128)(2,1)} %copy-done.7, bf16[2,256,128]{2,1,0:T(8,128)(2,1)} %copy-done.8, bf16[2,256,128]{2,1,0:T(8,128)(2,1)} %copy-done.4, ...), custom_call_target="tpu_custom_call" | custom-call | tf_op jit(solution)/shard_map/pallas_call | solution.py:277
  (121 shorter events, 6.6 us)
Async XLA Ops:
  0.0 0.7 copy-start.12
  2.6 0.7 copy-start.14
  2.6 0.7 copy-start.15
  2.6 0.7 copy-start.16
  10.0 8.6 %collective-permute-start = (bf16[8,256,128]{2,1,0:T(8,128)(2,1)}, bf16[8,256,128]{2,1,0:T(8,128)(2,1)S(1)}, u32[]{:S(2)}, u32[]{:S(2)}) collective-permute-start(bf16[8,256,128]{2,1,0:T(8,128)(2,1)} %get-tuple-element.18), channel_id=1, source_target_pairs={{0,16},{16,0},{1,17},{17,1},{2,18},{18,2},{3,19},{19,3},{4,20},{20... | collective-permute-start | bytes 1572872 | tf_op jit(solution)/shard_map/ppermute | solution.py:286
  10.6 6.5 %copy-start.17 = (s32[8]{0:T(128)S(1)}, s32[8]{0:T(128)}, u32[]{:S(2)}) copy-start(s32[8]{0:T(128)} %constant.81.clone) | copy-start | bytes 100
  10.6 7.8 %copy-start.2 = (bf16[8,256,128]{2,1,0:T(8,128)(2,1)S(1)}, bf16[8,256,128]{2,1,0:T(8,128)(2,1)}, u32[]{:S(2)}) copy-start(bf16[8,256,128]{2,1,0:T(8,128)(2,1)} %get-tuple-element.17) | copy-start | bytes 1572868
  17.1 1.4 copy-start.1
  17.1 2.9 %collective-permute-start.2 = (bf16[8,2,256,128]{3,2,1,0:T(8,128)(2,1)}, bf16[8,2,256,128]{3,2,1,0:T(8,128)(2,1)S(1)}, u32[]{:S(2)}, u32[]{:S(2)}) collective-permute-start(bf16[8,2,256,128]{3,2,1,0:T(8,128)(2,1)} %get-tuple-element.20), channel_id=1, source_target_pairs={{0,16},{16,0},{1,17},{17,1},{2,18},{18,2},{3,19},{19,3},{4,20},{20... | collective-permute-start | bytes 3145736 | tf_op jit(solution)/shard_map/ppermute | solution.py:286
  20.1 48.6 %collective-permute-start.3 = (bf16[2,2,256,128]{3,2,1,0:T(8,128)(2,1)S(1)}, bf16[2,2,256,128]{3,2,1,0:T(8,128)(2,1)S(1)}, u32[]{:S(2)}, u32[]{:S(2)}) collective-permute-start(bf16[2,2,256,128]{3,2,1,0:T(8,128)(2,1)S(1)} %pad_maximum_fusion.4), channel_id=1, source_target_pairs={{0,224},{32,0},{64,32},{96,64},{128,96},{160,128},{192,160},{224,1... | collective-permute-start | bytes 786440 | tf_op jit(solution)/shard_map/ppermute | solution.py:290
  25.7 44.9 %collective-permute-start.4 = (bf16[2,2,256,128]{3,2,1,0:T(8,128)(2,1)S(1)}, bf16[2,2,256,128]{3,2,1,0:T(8,128)(2,1)S(1)}, u32[]{:S(2)}, u32[]{:S(2)}) collective-permute-start(bf16[2,2,256,128]{3,2,1,0:T(8,128)(2,1)S(1)} %pad_maximum_fusion.5), channel_id=1, source_target_pairs={{0,32},{32,64},{64,96},{96,128},{128,160},{160,192},{192,224},{224... | collective-permute-start | bytes 786440 | tf_op jit(solution)/shard_map/ppermute | solution.py:290
  25.9 37.0 %collective-permute-start.9 = (bf16[2,2,256,128]{3,2,1,0:T(8,128)(2,1)S(1)}, bf16[2,2,256,128]{3,2,1,0:T(8,128)(2,1)S(1)}, u32[]{:S(2)}, u32[]{:S(2)}) collective-permute-start(bf16[2,2,256,128]{3,2,1,0:T(8,128)(2,1)S(1)} %pad_maximum_fusion.8), channel_id=1, source_target_pairs={{0,160},{32,192},{64,224},{96,0},{128,32},{160,64},{192,96},{224,1... | collective-permute-start | bytes 786440 | tf_op jit(solution)/shard_map/ppermute | solution.py:290
  28.3 35.7 %collective-permute-start.10 = (bf16[2,2,256,128]{3,2,1,0:T(8,128)(2,1)S(1)}, bf16[2,2,256,128]{3,2,1,0:T(8,128)(2,1)S(1)}, u32[]{:S(2)}, u32[]{:S(2)}) collective-permute-start(bf16[2,2,256,128]{3,2,1,0:T(8,128)(2,1)S(1)} %pad_maximum_fusion.9), channel_id=1, source_target_pairs={{0,96},{32,128},{64,160},{96,192},{128,224},{160,0},{192,32},{224,... | collective-permute-start | bytes 786440 | tf_op jit(solution)/shard_map/ppermute | solution.py:290
  29.3 27.2 %collective-permute-start.12 = (bf16[2,2,256,128]{3,2,1,0:T(8,128)(2,1)S(1)}, bf16[2,2,256,128]{3,2,1,0:T(8,128)(2,1)S(1)}, u32[]{:S(2)}, u32[]{:S(2)}) collective-permute-start(bf16[2,2,256,128]{3,2,1,0:T(8,128)(2,1)S(1)} %pad_maximum_fusion.10), channel_id=1, source_target_pairs={{0,128},{32,160},{64,192},{96,224},{128,0},{160,32},{192,64},{224,... | collective-permute-start | bytes 786440 | tf_op jit(solution)/shard_map/ppermute | solution.py:290
  56.5 19.7 %collective-permute-start.6 = (bf16[2,2,256,128]{3,2,1,0:T(8,128)(2,1)S(1)}, bf16[2,2,256,128]{3,2,1,0:T(8,128)(2,1)S(1)}, u32[]{:S(2)}, u32[]{:S(2)}) collective-permute-start(bf16[2,2,256,128]{3,2,1,0:T(8,128)(2,1)S(1)} %pad_maximum_fusion.6), channel_id=1, source_target_pairs={{0,192},{32,224},{64,0},{96,32},{128,64},{160,96},{192,128},{224,1... | collective-permute-start | bytes 786440 | tf_op jit(solution)/shard_map/ppermute | solution.py:290
  62.8 15.1 %collective-permute-start.7 = (bf16[2,2,256,128]{3,2,1,0:T(8,128)(2,1)S(1)}, bf16[2,2,256,128]{3,2,1,0:T(8,128)(2,1)S(1)}, u32[]{:S(2)}, u32[]{:S(2)}) collective-permute-start(bf16[2,2,256,128]{3,2,1,0:T(8,128)(2,1)S(1)} %pad_maximum_fusion.7), channel_id=1, source_target_pairs={{0,64},{32,96},{64,128},{96,160},{128,192},{160,224},{192,0},{224,... | collective-permute-start | bytes 786440 | tf_op jit(solution)/shard_map/ppermute | solution.py:290
  64.0 34.3 %collective-permute-start.17 = (bf16[2,2,2,256,128]{4,3,2,1,0:T(8,128)(2,1)S(1)}, bf16[2,2,2,256,128]{4,3,2,1,0:T(8,128)(2,1)S(1)}, u32[]{:S(2)}, u32[]{:S(2)}) collective-permute-start(bf16[2,2,2,256,128]{4,3,2,1,0:T(8,128)(2,1)S(1)} %pad_maximum_fusion.3.refs_7_), channel_id=1, source_target_pairs={{1,0},{2,1},{3,2},{4,3},{5,4},{6,5},{7,6},{8,7},{9,8},{10,9},{11,1... | collective-permute-start | bytes 1572872 | tf_op jit(solution)/shard_map/ppermute | solution.py:310
  68.7 31.5 %collective-permute-start.13 = (bf16[2,2,2,256,128]{4,3,2,1,0:T(8,128)(2,1)S(1)}, bf16[2,2,2,256,128]{4,3,2,1,0:T(8,128)(2,1)S(1)}, u32[]{:S(2)}, u32[]{:S(2)}) collective-permute-start(bf16[2,2,2,256,128]{4,3,2,1,0:T(8,128)(2,1)S(1)} %pad_maximum_fusion.3.refs_7_), channel_id=1, source_target_pairs={{0,1},{1,2},{2,3},{3,4},{4,5},{5,6},{6,7},{7,8},{8,9},{9,10},{10,1... | collective-permute-start | bytes 1572872 | tf_op jit(solution)/shard_map/ppermute | solution.py:309
  70.6 35.1 %collective-permute-start.16 = (bf16[2,2,2,256,128]{4,3,2,1,0:T(8,128)(2,1)S(1)}, bf16[2,2,2,256,128]{4,3,2,1,0:T(8,128)(2,1)S(1)}, u32[]{:S(2)}, u32[]{:S(2)}) collective-permute-start(bf16[2,2,2,256,128]{4,3,2,1,0:T(8,128)(2,1)S(1)} %pad_maximum_fusion.2.refs_6_), channel_id=1, source_target_pairs={{1,0},{2,1},{3,2},{4,3},{5,4},{6,5},{7,6},{8,7},{9,8},{10,9},{11,1... | collective-permute-start | bytes 1572872 | tf_op jit(solution)/shard_map/ppermute | solution.py:310
  76.2 11.0 %collective-permute-start.23 = (bf16[2,256,128]{2,1,0:T(8,128)(2,1)S(1)}, bf16[2,256,128]{2,1,0:T(8,128)(2,1)S(1)}, u32[]{:S(2)}, u32[]{:S(2)}) collective-permute-start(bf16[2,256,128]{2,1,0:T(8,128)(2,1)S(1)} %pad_maximum_fusion.15), channel_id=1, source_target_pairs={{0,96},{32,128},{64,160},{96,192},{128,224},{160,0},{192,32},{224,... | collective-permute-start | bytes 393224 | tf_op jit(solution)/shard_map/ppermute | solution.py:290
  78.0 16.3 %collective-permute-start.24 = (bf16[2,256,128]{2,1,0:T(8,128)(2,1)S(1)}, bf16[2,256,128]{2,1,0:T(8,128)(2,1)S(1)}, u32[]{:S(2)}, u32[]{:S(2)}) collective-permute-start(bf16[2,256,128]{2,1,0:T(8,128)(2,1)S(1)} %pad_maximum_fusion.16), channel_id=1, source_target_pairs={{0,64},{32,96},{64,128},{96,160},{128,192},{160,224},{192,0},{224,... | collective-permute-start | bytes 393224 | tf_op jit(solution)/shard_map/ppermute | solution.py:290
  87.2 20.8 %collective-permute-start.11 = (bf16[2,2,2,256,128]{4,3,2,1,0:T(8,128)(2,1)S(1)}, bf16[2,2,2,256,128]{4,3,2,1,0:T(8,128)(2,1)S(1)}, u32[]{:S(2)}, u32[]{:S(2)}) collective-permute-start(bf16[2,2,2,256,128]{4,3,2,1,0:T(8,128)(2,1)S(1)} %pad_maximum_fusion.2.refs_6_), channel_id=1, source_target_pairs={{0,1},{1,2},{2,3},{3,4},{4,5},{5,6},{6,7},{7,8},{8,9},{9,10},{10,1... | collective-permute-start | bytes 1572872 | tf_op jit(solution)/shard_map/ppermute | solution.py:309
  94.3 13.8 %collective-permute-start.15 = (bf16[2,2,2,256,128]{4,3,2,1,0:T(8,128)(2,1)S(1)}, bf16[2,2,2,256,128]{4,3,2,1,0:T(8,128)(2,1)S(1)}, u32[]{:S(2)}, u32[]{:S(2)}) collective-permute-start(bf16[2,2,2,256,128]{4,3,2,1,0:T(8,128)(2,1)S(1)} %pad_maximum_fusion.1.refs_5_), channel_id=1, source_target_pairs={{1,0},{2,1},{3,2},{4,3},{5,4},{6,5},{7,6},{8,7},{9,8},{10,9},{11,1... | collective-permute-start | bytes 1572872 | tf_op jit(solution)/shard_map/ppermute | solution.py:310
  98.3 16.4 %collective-permute-start.8 = (bf16[2,2,2,256,128]{4,3,2,1,0:T(8,128)(2,1)S(1)}, bf16[2,2,2,256,128]{4,3,2,1,0:T(8,128)(2,1)S(1)}, u32[]{:S(2)}, u32[]{:S(2)}) collective-permute-start(bf16[2,2,2,256,128]{4,3,2,1,0:T(8,128)(2,1)S(1)} %pad_maximum_fusion.1.refs_5_), channel_id=1, source_target_pairs={{0,1},{1,2},{2,3},{3,4},{4,5},{5,6},{6,7},{7,8},{8,9},{9,10},{10,1... | collective-permute-start | bytes 1572872 | tf_op jit(solution)/shard_map/ppermute | solution.py:309
  100.2 18.7 %collective-permute-start.14 = (bf16[2,2,2,256,128]{4,3,2,1,0:T(8,128)(2,1)S(1)}, bf16[2,2,2,256,128]{4,3,2,1,0:T(8,128)(2,1)S(1)}, u32[]{:S(2)}, u32[]{:S(2)}) collective-permute-start(bf16[2,2,2,256,128]{4,3,2,1,0:T(8,128)(2,1)S(1)} %pad_maximum_fusion.refs_4_), channel_id=1, source_target_pairs={{1,0},{2,1},{3,2},{4,3},{5,4},{6,5},{7,6},{8,7},{9,8},{10,9},{11,1... | collective-permute-start | bytes 1572872 | tf_op jit(solution)/shard_map/ppermute | solution.py:310
  105.7 19.6 %collective-permute-start.5 = (bf16[2,2,2,256,128]{4,3,2,1,0:T(8,128)(2,1)S(1)}, bf16[2,2,2,256,128]{4,3,2,1,0:T(8,128)(2,1)S(1)}, u32[]{:S(2)}, u32[]{:S(2)}) collective-permute-start(bf16[2,2,2,256,128]{4,3,2,1,0:T(8,128)(2,1)S(1)} %pad_maximum_fusion.refs_4_), channel_id=1, source_target_pairs={{0,1},{1,2},{2,3},{3,4},{4,5},{5,6},{6,7},{7,8},{8,9},{9,10},{10,1... | collective-permute-start | bytes 1572872 | tf_op jit(solution)/shard_map/ppermute | solution.py:309
  108.0 32.9 %collective-permute-start.1 = (bf16[2,256,128]{2,1,0:T(8,128)(2,1)S(1)}, bf16[2,256,128]{2,1,0:T(8,128)(2,1)S(1)}, u32[]{:S(2)}, u32[]{:S(2)}) collective-permute-start(bf16[2,256,128]{2,1,0:T(8,128)(2,1)S(1)} %pad_maximum_fusion.12), channel_id=1, source_target_pairs={{0,192},{32,224},{64,0},{96,32},{128,64},{160,96},{192,128},{224,1... | collective-permute-start | bytes 393224 | tf_op jit(solution)/shard_map/ppermute | solution.py:290
  108.1 48.7 %collective-permute-start.19 = (bf16[2,256,128]{2,1,0:T(8,128)(2,1)S(1)}, bf16[2,256,128]{2,1,0:T(8,128)(2,1)S(1)}, u32[]{:S(2)}, u32[]{:S(2)}) collective-permute-start(bf16[2,256,128]{2,1,0:T(8,128)(2,1)S(1)} %pad_maximum_fusion.13), channel_id=1, source_target_pairs={{0,128},{32,160},{64,192},{96,224},{128,0},{160,32},{192,64},{224,... | collective-permute-start | bytes 393224 | tf_op jit(solution)/shard_map/ppermute | solution.py:290
  114.7 53.3 %collective-permute-start.20 = (bf16[2,256,128]{2,1,0:T(8,128)(2,1)S(1)}, bf16[2,256,128]{2,1,0:T(8,128)(2,1)S(1)}, u32[]{:S(2)}, u32[]{:S(2)}) collective-permute-start(bf16[2,256,128]{2,1,0:T(8,128)(2,1)S(1)} %pad_maximum_fusion.14), channel_id=1, source_target_pairs={{0,160},{32,192},{64,224},{96,0},{128,32},{160,64},{192,96},{224,1... | collective-permute-start | bytes 393224 | tf_op jit(solution)/shard_map/ppermute | solution.py:290
  118.9 85.3 %collective-permute-start.27 = (bf16[2,256,128]{2,1,0:T(8,128)(2,1)S(1)}, bf16[2,256,128]{2,1,0:T(8,128)(2,1)S(1)}, u32[]{:S(2)}, u32[]{:S(2)}) collective-permute-start(bf16[2,256,128]{2,1,0:T(8,128)(2,1)S(1)} %pad_maximum_fusion.17), channel_id=1, source_target_pairs={{0,32},{32,64},{64,96},{96,128},{128,160},{160,192},{192,224},{224... | collective-permute-start | bytes 393224 | tf_op jit(solution)/shard_map/ppermute | solution.py:290
  125.3 78.9 %collective-permute-start.28 = (bf16[2,256,128]{2,1,0:T(8,128)(2,1)S(1)}, bf16[2,256,128]{2,1,0:T(8,128)(2,1)S(1)}, u32[]{:S(2)}, u32[]{:S(2)}) collective-permute-start(bf16[2,256,128]{2,1,0:T(8,128)(2,1)S(1)} %pad_maximum_fusion.18), channel_id=1, source_target_pairs={{0,224},{32,0},{64,32},{96,64},{128,96},{160,128},{192,160},{224,1... | collective-permute-start | bytes 393224 | tf_op jit(solution)/shard_map/ppermute | solution.py:290
  140.9 55.7 %collective-permute-start.25 = (bf16[2,256,128]{2,1,0:T(8,128)(2,1)S(1)}, bf16[2,256,128]{2,1,0:T(8,128)(2,1)S(1)}, u32[]{:S(2)}, u32[]{:S(2)}) collective-permute-start(bf16[2,256,128]{2,1,0:T(8,128)(2,1)S(1)} %get-tuple-element.25), channel_id=1, source_target_pairs={{0,160},{32,192},{64,224},{96,0},{128,32},{160,64},{192,96},{224,1... | collective-permute-start | bytes 393224 | tf_op jit(solution)/shard_map/ppermute | solution.py:290
  156.7 20.9 %copy-start = (bf16[2,256,128]{2,1,0:T(8,128)(2,1)}, bf16[2,256,128]{2,1,0:T(8,128)(2,1)S(1)}, u32[]{:S(2)}) copy-start(bf16[2,256,128]{2,1,0:T(8,128)(2,1)S(1)} %get-tuple-element.21.refs_0_) | copy-start | bytes 393220
  156.8 39.8 %collective-permute-start.26 = (bf16[2,256,128]{2,1,0:T(8,128)(2,1)S(1)}, bf16[2,256,128]{2,1,0:T(8,128)(2,1)S(1)}, u32[]{:S(2)}, u32[]{:S(2)}) collective-permute-start(bf16[2,256,128]{2,1,0:T(8,128)(2,1)S(1)} %get-tuple-element.26), channel_id=1, source_target_pairs={{0,192},{32,224},{64,0},{96,32},{128,64},{160,96},{192,128},{224,1... | collective-permute-start | bytes 393224 | tf_op jit(solution)/shard_map/ppermute | solution.py:290
  167.9 9.7 %collective-permute-start.18 = (bf16[2,256,128]{2,1,0:T(8,128)(2,1)S(1)}, bf16[2,256,128]{2,1,0:T(8,128)(2,1)S(1)}, u32[]{:S(2)}, u32[]{:S(2)}) collective-permute-start(bf16[2,256,128]{2,1,0:T(8,128)(2,1)S(1)} %get-tuple-element.22), channel_id=1, source_target_pairs={{0,64},{32,96},{64,128},{96,160},{128,192},{160,224},{192,0},{224,... | collective-permute-start | bytes 393224 | tf_op jit(solution)/shard_map/ppermute | solution.py:290
  177.7 11.2 %copy-start.6 = (bf16[2,256,128]{2,1,0:T(8,128)(2,1)}, bf16[2,256,128]{2,1,0:T(8,128)(2,1)S(1)}, u32[]{:S(2)}) copy-start(bf16[2,256,128]{2,1,0:T(8,128)(2,1)S(1)} %collective-permute-done.18.refs_1_) | copy-start | bytes 393220
  177.7 11.1 %collective-permute-start.21 = (bf16[2,256,128]{2,1,0:T(8,128)(2,1)S(1)}, bf16[2,256,128]{2,1,0:T(8,128)(2,1)S(1)}, u32[]{:S(2)}, u32[]{:S(2)}) collective-permute-start(bf16[2,256,128]{2,1,0:T(8,128)(2,1)S(1)} %get-tuple-element.23), channel_id=1, source_target_pairs={{0,128},{32,160},{64,192},{96,224},{128,0},{160,32},{192,64},{224,... | collective-permute-start | bytes 393224 | tf_op jit(solution)/shard_map/ppermute | solution.py:290
  188.8 7.7 %copy-start.7 = (bf16[2,256,128]{2,1,0:T(8,128)(2,1)}, bf16[2,256,128]{2,1,0:T(8,128)(2,1)S(1)}, u32[]{:S(2)}) copy-start(bf16[2,256,128]{2,1,0:T(8,128)(2,1)S(1)} %collective-permute-done.21.refs_2_) | copy-start | bytes 393220
  188.8 7.7 %collective-permute-start.22 = (bf16[2,256,128]{2,1,0:T(8,128)(2,1)S(1)}, bf16[2,256,128]{2,1,0:T(8,128)(2,1)S(1)}, u32[]{:S(2)}, u32[]{:S(2)}) collective-permute-start(bf16[2,256,128]{2,1,0:T(8,128)(2,1)S(1)} %get-tuple-element.24), channel_id=1, source_target_pairs={{0,96},{32,128},{64,160},{96,192},{128,224},{160,0},{192,32},{224,... | collective-permute-start | bytes 393224 | tf_op jit(solution)/shard_map/ppermute | solution.py:290
  196.6 7.7 %copy-start.4 = (bf16[2,256,128]{2,1,0:T(8,128)(2,1)}, bf16[2,256,128]{2,1,0:T(8,128)(2,1)S(1)}, u32[]{:S(2)}) copy-start(bf16[2,256,128]{2,1,0:T(8,128)(2,1)S(1)} %collective-permute-done.25.refs_4_) | copy-start | bytes 393220
  196.6 23.6 %copy-start.5 = (bf16[2,256,128]{2,1,0:T(8,128)(2,1)}, bf16[2,256,128]{2,1,0:T(8,128)(2,1)S(1)}, u32[]{:S(2)}) copy-start(bf16[2,256,128]{2,1,0:T(8,128)(2,1)S(1)} %collective-permute-done.26.refs_5_) | copy-start | bytes 393220
  197.2 35.6 %collective-permute-start.31 = (bf16[6,256,128]{2,1,0:T(8,128)(2,1)S(1)}, bf16[6,256,128]{2,1,0:T(8,128)(2,1)S(1)}, u32[]{:S(2)}, u32[]{:S(2)}) collective-permute-start(bf16[6,256,128]{2,1,0:T(8,128)(2,1)S(1)} %slice_dynamic-update-slice_fusion), channel_id=1, source_target_pairs={{0,16},{16,0},{1,17},{17,1},{2,18},{18,2},{3,19},{19,3},{4,20},{20... | collective-permute-start | bytes 1179656 | tf_op jit(solution)/shard_map/ppermute | solution.py:286
  220.2 6.6 %collective-permute-start.29 = (bf16[2,256,128]{2,1,0:T(8,128)(2,1)S(1)}, bf16[2,256,128]{2,1,0:T(8,128)(2,1)S(1)}, u32[]{:S(2)}, u32[]{:S(2)}) collective-permute-start(bf16[2,256,128]{2,1,0:T(8,128)(2,1)S(1)} %get-tuple-element.27), channel_id=1, source_target_pairs={{0,224},{32,0},{64,32},{96,64},{128,96},{160,128},{192,160},{224,1... | collective-permute-start | bytes 393224 | tf_op jit(solution)/shard_map/ppermute | solution.py:290
  224.0 6.0 %collective-permute-start.30 = (bf16[2,256,128]{2,1,0:T(8,128)(2,1)S(1)}, bf16[2,256,128]{2,1,0:T(8,128)(2,1)S(1)}, u32[]{:S(2)}, u32[]{:S(2)}) collective-permute-start(bf16[2,256,128]{2,1,0:T(8,128)(2,1)S(1)} %get-tuple-element.28), channel_id=1, source_target_pairs={{0,32},{32,64},{64,96},{96,128},{128,160},{160,192},{192,224},{224... | collective-permute-start | bytes 393224 | tf_op jit(solution)/shard_map/ppermute | solution.py:290
  226.8 3.2 %copy-start.9 = (bf16[2,256,128]{2,1,0:T(8,128)(2,1)}, bf16[2,256,128]{2,1,0:T(8,128)(2,1)S(1)}, u32[]{:S(2)}) copy-start(bf16[2,256,128]{2,1,0:T(8,128)(2,1)S(1)} %collective-permute-done.29.refs_6_) | copy-start | bytes 393220
  230.0 0.7 copy-start.10
  230.6 2.1 collective-permute-start.32
  233.4 0.7 copy-start.3
  (3 other events, 2.0 us)
where the time goes:
time: 237 us
  starting transfers between devices  104 us (44%)
  Pallas kernels  66.8 us (28%)
  waiting for transfers between devices  55.7 us (24%)
  local copies, waits for them, and re-layouts  5.44 us (2%)
  other arithmetic  3.84 us (2%)
    ppermute x21, starting transfers between devices, z_shift(): return lax.ppermute(x, 'z', [(i, (i + k) % 8) for i in range(8)])  67.2 us
    pallas_call x4, Pallas kernels, attend(): pl.pallas_call(attend_body, out_shape=(block, block), in_specs=[SMEM, VME...  52.2 us
    ppermute x21, waiting for transfers between devices, z_shift(): return lax.ppermute(x, 'z', [(i, (i + k) % 8) for i in range(8)])  51.7 us
    ppermute x4, starting transfers between devices, with_neighbours(): after.append(lax.ppermute(piece, 'dp', backward))  19.5 us
    pallas_call x2, Pallas kernels, head_blocks(): pl.pallas_call(body, out_shape=(out, out), in_specs=[SMEM] + [VMEM] * (le...  11.8 us
    ppermute x4, starting transfers between devices, core_swap(): return lax.ppermute(x, 'c', [(0, 1), (1, 0)])  8.92 us
    ppermute x4, starting transfers between devices, with_neighbours(): before.append(lax.ppermute(piece, 'dp', forward))  8.81 us
  transfers between devices with their start and end apart: 33, of which 11 were waited for; matrix products, arithmetic and copies ran while one was open for 1% of the time, Pallas kernels for 25%

commit v1 on v0

--- a/solution.py
+++ b/solution.py
@@ -118,9 +118,8 @@
     scores, probs = (s0, s1), (p0, p1)
     low_all = sc[2] // TILE
     high_all = (sc[5] + TILE - 1) // TILE
-    for i in range(1, 4):
-        low_all = jnp.minimum(low_all, sc[2 + 4 * i] // TILE)
-        high_all = jnp.maximum(high_all, (sc[5 + 4 * i] + TILE - 1) // TILE)
+    low_all = jnp.minimum(low_all, sc[6] // TILE)
+    high_all = jnp.maximum(high_all, (sc[9] + TILE - 1) // TILE)
 
     def start(t, carry):
         pack = t // 8
@@ -143,8 +142,8 @@
             pltpu.make_async_copy(kv[0].at[0], buf.at[t], sem.at[t]).wait()
             flag[t] = 1
 
-    qbuf[0:2] = q0[...]
-    qbuf[2:4] = q1[...]
+    qbuf[0] = q0[...].reshape(TILE, 128)
+    qbuf[1] = q1[...].reshape(TILE, 128)
 
     def one(i, carry):
         base = 2 + 4 * i
@@ -175,7 +174,7 @@
             acc[...] = acc[...] * shrink + weigh(jnp.maximum(t - 1, low), probs[1 - parity])
             s = scores[parity][...]
             if masked:
-                row = lax.broadcasted_iota(jnp.int32, (TILE, SUB), 0)
+                row = lax.broadcasted_iota(jnp.int32, (TILE, TILE), 0)
                 key = (row ^ (core * SUB)) + t * TILE
                 s = jnp.where((key >= qse[i, 0:1, :]) & (key < qse[i, 1:2, :]), s, MASK_FLOOR)
             new_top = jnp.maximum(top, jnp.max(s, axis=0, keepdims=True))
@@ -205,29 +204,29 @@
             return lax.switch(which, kinds, carry)
 
         first = (
-            jnp.full((1, SUB), MASK_FLOOR, jnp.float32),
-            jnp.zeros((1, SUB), jnp.float32),
-            jnp.ones((1, SUB), jnp.float32),
+            jnp.full((1, TILE), MASK_FLOOR, jnp.float32),
+            jnp.zeros((1, TILE), jnp.float32),
+            jnp.ones((1, TILE), jnp.float32),
         )
         _, total, shrink = lax.fori_loop(low, high, loop, first)
 
-        def finish(source):
-            out = ((acc[...] * shrink + weigh(high - 1, source)) / total).T.astype(BF16)
-
-            @pl.when(i < 2)
-            def _():
-                o0[jnp.minimum(i, 1)] = out
-
-            @pl.when(i >= 2)
-            def _():
-                o1[jnp.maximum(i - 2, 0)] = out
-
-        last = lax.rem(high - 1 - low, 2)
-        pl.when(last == 0)(lambda: finish(p0))
-        pl.when(last == 1)(lambda: finish(p1))
-        return carry
-
-    lax.fori_loop(0, 4, one, 0)
+        @pl.when(lax.rem(high - 1 - low, 2) == 1)
+        def _():
+            p0[...] = p1[...]
+
+        out = ((acc[...] * shrink + weigh(high - 1, p0)) / total).T.astype(BF16)
+
+        @pl.when(i == 0)
+        def _():
+            o0[...] = out.reshape(2, SUB, 128)
+
+        @pl.when(i == 1)
+        def _():
+            o1[...] = out.reshape(2, SUB, 128)
+
+        return carry
+
+    lax.fori_loop(0, 2, one, 0)
 
     def drain(t, carry):
         ensure(t)
@@ -247,12 +246,12 @@
             pltpu.VMEM((24, 2, 2, SUB, 128), BF16),
             pltpu.SemaphoreType.DMA((24,)),
             pltpu.SMEM((24,), jnp.int32),
-            pltpu.VMEM((4, SUB, 128), BF16),
-            pltpu.VMEM((128, SUB), jnp.float32),
-            pltpu.VMEM((TILE, SUB), jnp.float32),
-            pltpu.VMEM((TILE, SUB), jnp.float32),
-            pltpu.VMEM((TILE, SUB), BF16),
-            pltpu.VMEM((TILE, SUB), BF16),
+            pltpu.VMEM((2, TILE, 128), BF16),
+            pltpu.VMEM((128, TILE), jnp.float32),
+            pltpu.VMEM((TILE, TILE), jnp.float32),
+            pltpu.VMEM((TILE, TILE), jnp.float32),
+            pltpu.VMEM((TILE, TILE), BF16),
+            pltpu.VMEM((TILE, TILE), BF16),
         ],
         compiler_params=pltpu.CompilerParams(vmem_limit_bytes=40 << 20),
         cost_estimate=pl.CostEstimate(
@@ -343,13 +342,17 @@
     base = pack_base - 4096
     began = jnp.max(jnp.where(tokens[:, None] >= starts[None, :], starts[None, :], 0), axis=1)
     ended = jnp.min(jnp.where(tokens[:, None] < ends[None, :], ends[None, :], 65536), axis=1)
-    qse = jnp.stack([(began - base).reshape(16, SUB), (ended - base).reshape(16, SUB)], axis=1)
-    bounds = qse[:, :, :: SUB - 1].reshape(16, 4)
+    began = (began - base).reshape(8, TILE)
+    ended = (ended - base).reshape(8, TILE)
+    qse = jnp.stack([began, ended], axis=1)
+    bounds = jnp.stack(
+        [began.min(axis=1), began.max(axis=1), ended.min(axis=1), ended.max(axis=1)], axis=1
+    )
 
     returned = []
     for n, (a, b) in enumerate(GROUPS):
-        sc = jnp.concatenate([pos, bounds[4 * n : 4 * n + 4].reshape(16)])
-        outs = attend(sc, queries[a], queries[b], qse[4 * n : 4 * n + 4], blocks)
+        sc = jnp.concatenate([pos, bounds[2 * n : 2 * n + 2].reshape(8)])
+        outs = attend(sc, queries[a], queries[b], qse[2 * n : 2 * n + 2], blocks)
         for rel, out in zip((a, b), outs):
             returned.append(z_shift(out, rel) if rel else out)
     swapped_a = core_swap(jnp.stack([r[1] for r in returned[:6]]))

time: 237 us -> 235 us (level); the launches traced: 237 us -> 232 us
  transfers between devices with their start and end apart: 33 -> 33, of which waited for: 11 -> 10; matrix products, arithmetic and copies ran while one was open for 1% -> 1% of each run, Pallas kernels for 25% -> 24%
where the time goes in v1:
time: 235 us; the launch traced here: 232 us
  starting transfers between devices  103 us (44%)
  Pallas kernels  64.5 us (27%)
  waiting for transfers between devices  54.1 us (23%)
  local copies, waits for them, and re-layouts  5.84 us (2%)
  other arithmetic  4.1 us (2%)
    ppermute x21, starting transfers between devices, z_shift(): return lax.ppermute(x, 'z', [(i, (i + k) % 8) for i in range(8)])  66.1 us
    ppermute x21, waiting for transfers between devices, z_shift(): return lax.ppermute(x, 'z', [(i, (i + k) % 8) for i in range(8)])  50.6 us
    pallas_call x4, Pallas kernels, attend(): pl.pallas_call(attend_body, out_shape=(block, block), in_specs=[SMEM, VME...  50 us
    ppermute x4, starting transfers between devices, with_neighbours(): after.append(lax.ppermute(piece, 'dp', backward))  19.5 us
    pallas_call x2, Pallas kernels, head_blocks(): pl.pallas_call(body, out_shape=(out, out), in_specs=[SMEM] + [VMEM] * (le...  11.8 us
    ppermute x4, starting transfers between devices, with_neighbours(): before.append(lax.ppermute(piece, 'dp', forward))  8.81 us
    ppermute x4, starting transfers between devices, core_swap(): return lax.ppermute(x, 'c', [(0, 1), (1, 0)])  8.08 us
    unnamed x42, local copies, waits for them, and re-layouts  4.71 us
  transfers between devices with their start and end apart: 33, of which 10 were waited for; matrix products, arithmetic and copies ran while one was open for 1% of the time, Pallas kernels for 24%

profile of v1, /device:TPU:5, one launch (start us, length us, event | category | flops | bytes accessed | tf_op | source)
XLA Modules:
  0.0 231.7 jit_solution(14368301190963094704)
XLA Ops:
  0.0 0.7 copy-done.12
  3.3 1.3 fusion
  4.6 5.3 %shard_map.109 = (bf16[8,256,128]{2,1,0:T(8,128)(2,1)}, bf16[8,256,128]{2,1,0:T(8,128)(2,1)}) custom-call(s32[2]{0:T(128)} %get-tuple-element.90.pos, bf16[256,2048]{1,0:T(8,128)(2,1)} %bitcast.47, f32[1,128]{1,0:T(1,128)} %bitcast.50, f32[256,128]{1,0:T(8,128)} %get-tuple-element.77.cos, f32[256,128]{1,0:T(8,128)} %get-tuple-element.76.sin), custom_call_target="tpu_custom_call" | custom-call | flops 2000000000 | bytes 4000000 | tf_op jit(solution)/shard_map/pallas_call | solution.py:103
  9.9 0.7 collective-permute-start
  10.6 6.4 %shard_map.110 = (bf16[8,2,256,128]{3,2,1,0:T(8,128)(2,1)}, bf16[8,2,256,128]{3,2,1,0:T(8,128)(2,1)}) custom-call(s32[2]{0:T(128)} %get-tuple-element.90.pos, bf16[256,2048]{1,0:T(8,128)(2,1)} %bitcast.48, bf16[256,2048]{1,0:T(8,128)(2,1)} %bitcast.49, f32[1,128]{1,0:T(1,128)} %bitcast.51, f32[256,128]{1,0:T(8,128)} %get-tuple-element.77.cos, ...), custom_call_target="tpu_custom_call" | custom-call | flops 2000000000 | bytes 4000000 | tf_op jit(solution)/shard_map/pallas_call | solution.py:103
  19.2 0.7 collective-permute-done.2
  20.0 5.7 %collective-permute-start.3 = (bf16[2,2,256,128]{3,2,1,0:T(8,128)(2,1)S(1)}, bf16[2,2,256,128]{3,2,1,0:T(8,128)(2,1)S(1)}, u32[]{:S(2)}, u32[]{:S(2)}) collective-permute-start(bf16[2,2,256,128]{3,2,1,0:T(8,128)(2,1)S(1)} %pad_maximum_fusion.4), channel_id=1, source_target_pairs={{0,224},{32,0},{64,32},{96,64},{128,96},{160,128},{192,160},{224,1... | collective-permute-start | bytes 786440 | tf_op jit(solution)/shard_map/ppermute | solution.py:289
  25.8 2.4 %collective-permute-start.9 = (bf16[2,2,256,128]{3,2,1,0:T(8,128)(2,1)S(1)}, bf16[2,2,256,128]{3,2,1,0:T(8,128)(2,1)S(1)}, u32[]{:S(2)}, u32[]{:S(2)}) collective-permute-start(bf16[2,2,256,128]{3,2,1,0:T(8,128)(2,1)S(1)} %pad_maximum_fusion.8), channel_id=1, source_target_pairs={{0,160},{32,192},{64,224},{96,0},{128,32},{160,64},{192,96},{224,1... | collective-permute-start | bytes 786440 | tf_op jit(solution)/shard_map/ppermute | solution.py:289
  28.3 1.0 collective-permute-start.10
  29.3 2.9 %collective-permute-start.12 = (bf16[2,2,256,128]{3,2,1,0:T(8,128)(2,1)S(1)}, bf16[2,2,256,128]{3,2,1,0:T(8,128)(2,1)S(1)}, u32[]{:S(2)}, u32[]{:S(2)}) collective-permute-start(bf16[2,2,256,128]{3,2,1,0:T(8,128)(2,1)S(1)} %pad_maximum_fusion.10), channel_id=1, source_target_pairs={{0,128},{32,160},{64,192},{96,224},{128,0},{160,32},{192,64},{224,... | collective-permute-start | bytes 786440 | tf_op jit(solution)/shard_map/ppermute | solution.py:289
  32.3 24.2 %collective-permute-done.12 = bf16[2,2,256,128]{3,2,1,0:T(8,128)(2,1)S(1)} collective-permute-done((bf16[2,2,256,128]{3,2,1,0:T(8,128)(2,1)S(1)}, bf16[2,2,256,128]{3,2,1,0:T(8,128)(2,1)S(1)}, u32[]{:S(2)}, u32[]{:S(2)}) %collective-permute-start.12) | collective-permute-done | bytes 262176 | tf_op jit(solution)/shard_map/ppermute | solution.py:289
  56.5 6.3 %collective-permute-start.6 = (bf16[2,2,256,128]{3,2,1,0:T(8,128)(2,1)S(1)}, bf16[2,2,256,128]{3,2,1,0:T(8,128)(2,1)S(1)}, u32[]{:S(2)}, u32[]{:S(2)}) collective-permute-start(bf16[2,2,256,128]{3,2,1,0:T(8,128)(2,1)S(1)} %pad_maximum_fusion.6), channel_id=1, source_target_pairs={{0,192},{32,224},{64,0},{96,32},{128,64},{160,96},{192,128},{224,1... | collective-permute-start | bytes 786440 | tf_op jit(solution)/shard_map/ppermute | solution.py:289
  62.8 1.2 collective-permute-start.7
  64.0 4.6 %collective-permute-start.17 = (bf16[2,2,2,256,128]{4,3,2,1,0:T(8,128)(2,1)S(1)}, bf16[2,2,2,256,128]{4,3,2,1,0:T(8,128)(2,1)S(1)}, u32[]{:S(2)}, u32[]{:S(2)}) collective-permute-start(bf16[2,2,2,256,128]{4,3,2,1,0:T(8,128)(2,1)S(1)} %pad_maximum_fusion.3.refs_7_), channel_id=1, source_target_pairs={{1,0},{2,1},{3,2},{4,3},{5,4},{6,5},{7,6},{8,7},{9,8},{10,9},{11,1... | collective-permute-start | bytes 1572872 | tf_op jit(solution)/shard_map/ppermute | solution.py:309
  68.7 1.9 collective-permute-start.13
  70.6 5.5 %collective-permute-start.16 = (bf16[2,2,2,256,128]{4,3,2,1,0:T(8,128)(2,1)S(1)}, bf16[2,2,2,256,128]{4,3,2,1,0:T(8,128)(2,1)S(1)}, u32[]{:S(2)}, u32[]{:S(2)}) collective-permute-start(bf16[2,2,2,256,128]{4,3,2,1,0:T(8,128)(2,1)S(1)} %pad_maximum_fusion.2.refs_6_), channel_id=1, source_target_pairs={{1,0},{2,1},{3,2},{4,3},{5,4},{6,5},{7,6},{8,7},{9,8},{10,9},{11,1... | collective-permute-start | bytes 1572872 | tf_op jit(solution)/shard_map/ppermute | solution.py:309
  76.2 1.8 collective-permute-start.23
  77.9 2.0 collective-permute-start.24
  80.0 7.1 %collective-permute-done.23.q0 = bf16[2,256,128]{2,1,0:T(8,128)(2,1)S(1)} collective-permute-done((bf16[2,256,128]{2,1,0:T(8,128)(2,1)S(1)}, bf16[2,256,128]{2,1,0:T(8,128)(2,1)S(1)}, u32[]{:S(2)}, u32[]{:S(2)}) %collective-permute-start.23) | collective-permute-done | bytes 131104 | tf_op jit(solution)/shard_map/ppermute | solution.py:289
  87.1 2.9 %collective-permute-start.11 = (bf16[2,2,2,256,128]{4,3,2,1,0:T(8,128)(2,1)S(1)}, bf16[2,2,2,256,128]{4,3,2,1,0:T(8,128)(2,1)S(1)}, u32[]{:S(2)}, u32[]{:S(2)}) collective-permute-start(bf16[2,2,2,256,128]{4,3,2,1,0:T(8,128)(2,1)S(1)} %pad_maximum_fusion.2.refs_6_), channel_id=1, source_target_pairs={{0,1},{1,2},{2,3},{3,4},{4,5},{5,6},{6,7},{7,8},{8,9},{9,10},{10,1... | collective-permute-start | bytes 1572872 | tf_op jit(solution)/shard_map/ppermute | solution.py:308
  90.0 4.3 %collective-permute-done.24.q1 = bf16[2,256,128]{2,1,0:T(8,128)(2,1)S(1)} collective-permute-done((bf16[2,256,128]{2,1,0:T(8,128)(2,1)S(1)}, bf16[2,256,128]{2,1,0:T(8,128)(2,1)S(1)}, u32[]{:S(2)}, u32[]{:S(2)}) %collective-permute-start.24) | collective-permute-done | bytes 131104 | tf_op jit(solution)/shard_map/ppermute | solution.py:289
  94.3 4.0 %collective-permute-start.15 = (bf16[2,2,2,256,128]{4,3,2,1,0:T(8,128)(2,1)S(1)}, bf16[2,2,2,256,128]{4,3,2,1,0:T(8,128)(2,1)S(1)}, u32[]{:S(2)}, u32[]{:S(2)}) collective-permute-start(bf16[2,2,2,256,128]{4,3,2,1,0:T(8,128)(2,1)S(1)} %pad_maximum_fusion.1.refs_5_), channel_id=1, source_target_pairs={{1,0},{2,1},{3,2},{4,3},{5,4},{6,5},{7,6},{8,7},{9,8},{10,9},{11,1... | collective-permute-start | bytes 1572872 | tf_op jit(solution)/shard_map/ppermute | solution.py:309
  98.3 1.9 collective-permute-start.8
  100.2 5.5 %collective-permute-start.14 = (bf16[2,2,2,256,128]{4,3,2,1,0:T(8,128)(2,1)S(1)}, bf16[2,2,2,256,128]{4,3,2,1,0:T(8,128)(2,1)S(1)}, u32[]{:S(2)}, u32[]{:S(2)}) collective-permute-start(bf16[2,2,2,256,128]{4,3,2,1,0:T(8,128)(2,1)S(1)} %pad_maximum_fusion.refs_4_), channel_id=1, source_target_pairs={{1,0},{2,1},{3,2},{4,3},{5,4},{6,5},{7,6},{8,7},{9,8},{10,9},{11,1... | collective-permute-start | bytes 1572872 | tf_op jit(solution)/shard_map/ppermute | solution.py:309
  105.7 2.1 collective-permute-start.5
  108.0 6.6 %collective-permute-start.19 = (bf16[2,256,128]{2,1,0:T(8,128)(2,1)S(1)}, bf16[2,256,128]{2,1,0:T(8,128)(2,1)S(1)}, u32[]{:S(2)}, u32[]{:S(2)}) collective-permute-start(bf16[2,256,128]{2,1,0:T(8,128)(2,1)S(1)} %pad_maximum_fusion.13), channel_id=1, source_target_pairs={{0,128},{32,160},{64,192},{96,224},{128,0},{160,32},{192,64},{224,... | collective-permute-start | bytes 393224 | tf_op jit(solution)/shard_map/ppermute | solution.py:289
  114.6 3.9 %collective-permute-start.20 = (bf16[2,256,128]{2,1,0:T(8,128)(2,1)S(1)}, bf16[2,256,128]{2,1,0:T(8,128)(2,1)S(1)}, u32[]{:S(2)}, u32[]{:S(2)}) collective-permute-start(bf16[2,256,128]{2,1,0:T(8,128)(2,1)S(1)} %pad_maximum_fusion.14), channel_id=1, source_target_pairs={{0,160},{32,192},{64,224},{96,0},{128,32},{160,64},{192,96},{224,1... | collective-permute-start | bytes 393224 | tf_op jit(solution)/shard_map/ppermute | solution.py:289
  118.9 5.1 %collective-permute-start.27 = (bf16[2,256,128]{2,1,0:T(8,128)(2,1)S(1)}, bf16[2,256,128]{2,1,0:T(8,128)(2,1)S(1)}, u32[]{:S(2)}, u32[]{:S(2)}) collective-permute-start(bf16[2,256,128]{2,1,0:T(8,128)(2,1)S(1)} %pad_maximum_fusion.17), channel_id=1, source_target_pairs={{0,32},{32,64},{64,96},{96,128},{128,160},{160,192},{192,224},{224... | collective-permute-start | bytes 393224 | tf_op jit(solution)/shard_map/ppermute | solution.py:289
  124.0 1.3 collective-permute-done.5.refs_0_
  125.3 3.3 %collective-permute-start.28 = (bf16[2,256,128]{2,1,0:T(8,128)(2,1)S(1)}, bf16[2,256,128]{2,1,0:T(8,128)(2,1)S(1)}, u32[]{:S(2)}, u32[]{:S(2)}) collective-permute-start(bf16[2,256,128]{2,1,0:T(8,128)(2,1)S(1)} %pad_maximum_fusion.18), channel_id=1, source_target_pairs={{0,224},{32,0},{64,32},{96,64},{128,96},{160,128},{192,160},{224,1... | collective-permute-start | bytes 393224 | tf_op jit(solution)/shard_map/ppermute | solution.py:289
  128.6 12.7 %shard_map.113 = (bf16[2,256,128]{2,1,0:T(8,128)(2,1)S(1)}, bf16[2,256,128]{2,1,0:T(8,128)(2,1)S(1)}) custom-call(s32[10]{0:T(128)S(1)} %get-tuple-element.87.sc, bf16[2,256,128]{2,1,0:T(8,128)(2,1)S(1)} %collective-permute-done.23.q0, bf16[2,256,128]{2,1,0:T(8,128)(2,1)S(1)} %collective-permute-done.24.q1, s32[2,2,512]{2,1,0:T(2,128)S(1)} %get-tuple-element.75.qse, ...), custom_call_target="tpu_custom_call" | custom-call | flops 12000000000 | bytes 8000000 | tf_op jit(solution)/shard_map/pallas_call | solution.py:240
  141.2 3.0 %collective-permute-start.25 = (bf16[2,256,128]{2,1,0:T(8,128)(2,1)S(1)}, bf16[2,256,128]{2,1,0:T(8,128)(2,1)S(1)}, u32[]{:S(2)}, u32[]{:S(2)}) collective-permute-start(bf16[2,256,128]{2,1,0:T(8,128)(2,1)S(1)} %get-tuple-element.25), channel_id=1, source_target_pairs={{0,160},{32,192},{64,224},{96,0},{128,32},{160,64},{192,96},{224,1... | collective-permute-start | bytes 393224 | tf_op jit(solution)/shard_map/ppermute | solution.py:289
  144.2 15.2 %shard_map.111 = (bf16[2,256,128]{2,1,0:T(8,128)(2,1)S(1)}, bf16[2,256,128]{2,1,0:T(8,128)(2,1)S(1)}) custom-call(s32[10]{0:T(128)S(1)} %get-tuple-element.89.sc, bf16[2,256,128]{2,1,0:T(8,128)(2,1)S(1)} %pad_maximum_fusion.11.q0, bf16[2,256,128]{2,1,0:T(8,128)(2,1)S(1)} %collective-permute-done.1.q1, s32[2,2,512]{2,1,0:T(2,128)S(1)} %get-tuple-element.73.qse, ...), custom_call_target="tpu_custom_call" | custom-call | flops 12000000000 | bytes 8000000 | tf_op jit(solution)/shard_map/pallas_call | solution.py:240
  159.5 5.5 %collective-permute-start.26 = (bf16[2,256,128]{2,1,0:T(8,128)(2,1)S(1)}, bf16[2,256,128]{2,1,0:T(8,128)(2,1)S(1)}, u32[]{:S(2)}, u32[]{:S(2)}) collective-permute-start(bf16[2,256,128]{2,1,0:T(8,128)(2,1)S(1)} %get-tuple-element.26), channel_id=1, source_target_pairs={{0,192},{32,224},{64,0},{96,32},{128,64},{160,96},{192,128},{224,1... | collective-permute-start | bytes 393224 | tf_op jit(solution)/shard_map/ppermute | solution.py:289
  164.9 8.8 %shard_map.112 = (bf16[2,256,128]{2,1,0:T(8,128)(2,1)S(1)}, bf16[2,256,128]{2,1,0:T(8,128)(2,1)S(1)}) custom-call(s32[10]{0:T(128)S(1)} %get-tuple-element.88.sc, bf16[2,256,128]{2,1,0:T(8,128)(2,1)S(1)} %collective-permute-done.19.q0, bf16[2,256,128]{2,1,0:T(8,128)(2,1)S(1)} %collective-permute-done.20.q1, s32[2,2,512]{2,1,0:T(2,128)S(1)} %get-tuple-element.74.qse, ...), custom_call_target="tpu_custom_call" | custom-call | flops 12000000000 | bytes 8000000 | tf_op jit(solution)/shard_map/pallas_call | solution.py:240
  173.8 7.0 %collective-permute-start.21 = (bf16[2,256,128]{2,1,0:T(8,128)(2,1)S(1)}, bf16[2,256,128]{2,1,0:T(8,128)(2,1)S(1)}, u32[]{:S(2)}, u32[]{:S(2)}) collective-permute-start(bf16[2,256,128]{2,1,0:T(8,128)(2,1)S(1)} %get-tuple-element.23), channel_id=1, source_target_pairs={{0,128},{32,160},{64,192},{96,224},{128,0},{160,32},{192,64},{224,... | collective-permute-start | bytes 393224 | tf_op jit(solution)/shard_map/ppermute | solution.py:289
  180.8 2.3 %collective-permute-done.21.refs_2_ = bf16[2,256,128]{2,1,0:T(8,128)(2,1)S(1)} collective-permute-done((bf16[2,256,128]{2,1,0:T(8,128)(2,1)S(1)}, bf16[2,256,128]{2,1,0:T(8,128)(2,1)S(1)}, u32[]{:S(2)}, u32[]{:S(2)}) %collective-permute-start.21) | collective-permute-done | bytes 131104 | tf_op jit(solution)/shard_map/ppermute | solution.py:289
  183.7 8.9 %collective-permute-done.22.refs_3_ = bf16[2,256,128]{2,1,0:T(8,128)(2,1)S(1)} collective-permute-done((bf16[2,256,128]{2,1,0:T(8,128)(2,1)S(1)}, bf16[2,256,128]{2,1,0:T(8,128)(2,1)S(1)}, u32[]{:S(2)}, u32[]{:S(2)}) %collective-permute-start.22) | collective-permute-done | bytes 131104 | tf_op jit(solution)/shard_map/ppermute | solution.py:289
  193.3 6.4 %collective-permute-start.31 = (bf16[6,256,128]{2,1,0:T(8,128)(2,1)S(1)}, bf16[6,256,128]{2,1,0:T(8,128)(2,1)S(1)}, u32[]{:S(2)}, u32[]{:S(2)}) collective-permute-start(bf16[6,256,128]{2,1,0:T(8,128)(2,1)S(1)} %slice_dynamic-update-slice_fusion), channel_id=1, source_target_pairs={{0,16},{16,0},{1,17},{17,1},{2,18},{18,2},{3,19},{19,3},{4,20},{20... | collective-permute-start | bytes 1179656 | tf_op jit(solution)/shard_map/ppermute | solution.py:285
  199.7 13.3 %shard_map.114 = (bf16[2,256,128]{2,1,0:T(8,128)(2,1)S(1)}, bf16[2,256,128]{2,1,0:T(8,128)(2,1)S(1)}) custom-call(s32[10]{0:T(128)S(1)} %get-tuple-element.38.sc, bf16[2,256,128]{2,1,0:T(8,128)(2,1)S(1)} %collective-permute-done.27.q0, bf16[2,256,128]{2,1,0:T(8,128)(2,1)S(1)} %collective-permute-done.28.q1, s32[2,2,512]{2,1,0:T(2,128)S(1)} %get-tuple-element.72.qse, ...), custom_call_target="tpu_custom_call" | custom-call | flops 12000000000 | bytes 8000000 | tf_op jit(solution)/shard_map/pallas_call | solution.py:240
  213.1 5.7 %collective-permute-start.29 = (bf16[2,256,128]{2,1,0:T(8,128)(2,1)S(1)}, bf16[2,256,128]{2,1,0:T(8,128)(2,1)S(1)}, u32[]{:S(2)}, u32[]{:S(2)}) collective-permute-start(bf16[2,256,128]{2,1,0:T(8,128)(2,1)S(1)} %get-tuple-element.27), channel_id=1, source_target_pairs={{0,224},{32,0},{64,32},{96,64},{128,96},{160,128},{192,160},{224,1... | collective-permute-start | bytes 393224 | tf_op jit(solution)/shard_map/ppermute | solution.py:289
  218.8 2.3 %collective-permute-start.30 = (bf16[2,256,128]{2,1,0:T(8,128)(2,1)S(1)}, bf16[2,256,128]{2,1,0:T(8,128)(2,1)S(1)}, u32[]{:S(2)}, u32[]{:S(2)}) collective-permute-start(bf16[2,256,128]{2,1,0:T(8,128)(2,1)S(1)} %get-tuple-element.28), channel_id=1, source_target_pairs={{0,32},{32,64},{64,96},{96,128},{128,160},{160,192},{192,224},{224... | collective-permute-start | bytes 393224 | tf_op jit(solution)/shard_map/ppermute | solution.py:289
  221.1 3.8 %collective-permute-done.29.refs_6_ = bf16[2,256,128]{2,1,0:T(8,128)(2,1)S(1)} collective-permute-done((bf16[2,256,128]{2,1,0:T(8,128)(2,1)S(1)}, bf16[2,256,128]{2,1,0:T(8,128)(2,1)S(1)}, u32[]{:S(2)}, u32[]{:S(2)}) %collective-permute-start.29) | collective-permute-done | bytes 131104 | tf_op jit(solution)/shard_map/ppermute | solution.py:289
  225.6 1.0 collective-permute-start.32
  226.6 1.0 collective-permute-done.32.refs_9_
  227.6 0.7 copy-done.11
  228.3 0.7 copy-done.3
  229.0 2.7 %shard_map.115 = bf16[256,2048]{1,0:T(8,128)(2,1)} custom-call(s32[2]{0:T(128)} %get-tuple-element.90.pos, bf16[2,256,128]{2,1,0:T(8,128)(2,1)} %copy-done, bf16[2,256,128]{2,1,0:T(8,128)(2,1)} %copy-done.6, bf16[2,256,128]{2,1,0:T(8,128)(2,1)} %copy-done.7, bf16[2,256,128]{2,1,0:T(8,128)(2,1)} %copy-done.8, bf16[2,256,128]{2,1,0:T(8,128)(2,1)} %copy-done.4, ...), custom_call_target="tpu_custom_call" | custom-call | tf_op jit(solution)/shard_map/pallas_call | solution.py:276
  (128 shorter events, 7.7 us)
Async XLA Ops:
  0.0 0.7 copy-start.12
  2.6 0.7 copy-start.15
  2.7 0.7 copy-start.16
  9.9 9.2 %collective-permute-start = (bf16[8,256,128]{2,1,0:T(8,128)(2,1)}, bf16[8,256,128]{2,1,0:T(8,128)(2,1)S(1)}, u32[]{:S(2)}, u32[]{:S(2)}) collective-permute-start(bf16[8,256,128]{2,1,0:T(8,128)(2,1)} %get-tuple-element.18), channel_id=1, source_target_pairs={{0,16},{16,0},{1,17},{17,1},{2,18},{18,2},{3,19},{19,3},{4,20},{20... | collective-permute-start | bytes 1572872 | tf_op jit(solution)/shard_map/ppermute | solution.py:285
  10.6 6.4 %copy-start.17 = (s32[8]{0:T(128)S(1)}, s32[8]{0:T(128)}, u32[]{:S(2)}) copy-start(s32[8]{0:T(128)} %constant.81.clone) | copy-start | bytes 100
  10.6 8.4 %copy-start.2 = (bf16[8,256,128]{2,1,0:T(8,128)(2,1)S(1)}, bf16[8,256,128]{2,1,0:T(8,128)(2,1)}, u32[]{:S(2)}) copy-start(bf16[8,256,128]{2,1,0:T(8,128)(2,1)} %get-tuple-element.17) | copy-start | bytes 1572868
  17.0 2.0 copy-start.1
  17.0 2.9 %collective-permute-start.2 = (bf16[8,2,256,128]{3,2,1,0:T(8,128)(2,1)}, bf16[8,2,256,128]{3,2,1,0:T(8,128)(2,1)S(1)}, u32[]{:S(2)}, u32[]{:S(2)}) collective-permute-start(bf16[8,2,256,128]{3,2,1,0:T(8,128)(2,1)} %get-tuple-element.20), channel_id=1, source_target_pairs={{0,16},{16,0},{1,17},{17,1},{2,18},{18,2},{3,19},{19,3},{4,20},{20... | collective-permute-start | bytes 3145736 | tf_op jit(solution)/shard_map/ppermute | solution.py:285
  20.0 48.6 %collective-permute-start.3 = (bf16[2,2,256,128]{3,2,1,0:T(8,128)(2,1)S(1)}, bf16[2,2,256,128]{3,2,1,0:T(8,128)(2,1)S(1)}, u32[]{:S(2)}, u32[]{:S(2)}) collective-permute-start(bf16[2,2,256,128]{3,2,1,0:T(8,128)(2,1)S(1)} %pad_maximum_fusion.4), channel_id=1, source_target_pairs={{0,224},{32,0},{64,32},{96,64},{128,96},{160,128},{192,160},{224,1... | collective-permute-start | bytes 786440 | tf_op jit(solution)/shard_map/ppermute | solution.py:289
  25.7 44.9 %collective-permute-start.4 = (bf16[2,2,256,128]{3,2,1,0:T(8,128)(2,1)S(1)}, bf16[2,2,256,128]{3,2,1,0:T(8,128)(2,1)S(1)}, u32[]{:S(2)}, u32[]{:S(2)}) collective-permute-start(bf16[2,2,256,128]{3,2,1,0:T(8,128)(2,1)S(1)} %pad_maximum_fusion.5), channel_id=1, source_target_pairs={{0,32},{32,64},{64,96},{96,128},{128,160},{160,192},{192,224},{224... | collective-permute-start | bytes 786440 | tf_op jit(solution)/shard_map/ppermute | solution.py:289
  25.8 37.0 %collective-permute-start.9 = (bf16[2,2,256,128]{3,2,1,0:T(8,128)(2,1)S(1)}, bf16[2,2,256,128]{3,2,1,0:T(8,128)(2,1)S(1)}, u32[]{:S(2)}, u32[]{:S(2)}) collective-permute-start(bf16[2,2,256,128]{3,2,1,0:T(8,128)(2,1)S(1)} %pad_maximum_fusion.8), channel_id=1, source_target_pairs={{0,160},{32,192},{64,224},{96,0},{128,32},{160,64},{192,96},{224,1... | collective-permute-start | bytes 786440 | tf_op jit(solution)/shard_map/ppermute | solution.py:289
  28.3 35.7 %collective-permute-start.10 = (bf16[2,2,256,128]{3,2,1,0:T(8,128)(2,1)S(1)}, bf16[2,2,256,128]{3,2,1,0:T(8,128)(2,1)S(1)}, u32[]{:S(2)}, u32[]{:S(2)}) collective-permute-start(bf16[2,2,256,128]{3,2,1,0:T(8,128)(2,1)S(1)} %pad_maximum_fusion.9), channel_id=1, source_target_pairs={{0,96},{32,128},{64,160},{96,192},{128,224},{160,0},{192,32},{224,... | collective-permute-start | bytes 786440 | tf_op jit(solution)/shard_map/ppermute | solution.py:289
  29.3 27.2 %collective-permute-start.12 = (bf16[2,2,256,128]{3,2,1,0:T(8,128)(2,1)S(1)}, bf16[2,2,256,128]{3,2,1,0:T(8,128)(2,1)S(1)}, u32[]{:S(2)}, u32[]{:S(2)}) collective-permute-start(bf16[2,2,256,128]{3,2,1,0:T(8,128)(2,1)S(1)} %pad_maximum_fusion.10), channel_id=1, source_target_pairs={{0,128},{32,160},{64,192},{96,224},{128,0},{160,32},{192,64},{224,... | collective-permute-start | bytes 786440 | tf_op jit(solution)/shard_map/ppermute | solution.py:289
  56.5 19.7 %collective-permute-start.6 = (bf16[2,2,256,128]{3,2,1,0:T(8,128)(2,1)S(1)}, bf16[2,2,256,128]{3,2,1,0:T(8,128)(2,1)S(1)}, u32[]{:S(2)}, u32[]{:S(2)}) collective-permute-start(bf16[2,2,256,128]{3,2,1,0:T(8,128)(2,1)S(1)} %pad_maximum_fusion.6), channel_id=1, source_target_pairs={{0,192},{32,224},{64,0},{96,32},{128,64},{160,96},{192,128},{224,1... | collective-permute-start | bytes 786440 | tf_op jit(solution)/shard_map/ppermute | solution.py:289
  62.8 15.1 %collective-permute-start.7 = (bf16[2,2,256,128]{3,2,1,0:T(8,128)(2,1)S(1)}, bf16[2,2,256,128]{3,2,1,0:T(8,128)(2,1)S(1)}, u32[]{:S(2)}, u32[]{:S(2)}) collective-permute-start(bf16[2,2,256,128]{3,2,1,0:T(8,128)(2,1)S(1)} %pad_maximum_fusion.7), channel_id=1, source_target_pairs={{0,64},{32,96},{64,128},{96,160},{128,192},{160,224},{192,0},{224,... | collective-permute-start | bytes 786440 | tf_op jit(solution)/shard_map/ppermute | solution.py:289
  64.0 34.3 %collective-permute-start.17 = (bf16[2,2,2,256,128]{4,3,2,1,0:T(8,128)(2,1)S(1)}, bf16[2,2,2,256,128]{4,3,2,1,0:T(8,128)(2,1)S(1)}, u32[]{:S(2)}, u32[]{:S(2)}) collective-permute-start(bf16[2,2,2,256,128]{4,3,2,1,0:T(8,128)(2,1)S(1)} %pad_maximum_fusion.3.refs_7_), channel_id=1, source_target_pairs={{1,0},{2,1},{3,2},{4,3},{5,4},{6,5},{7,6},{8,7},{9,8},{10,9},{11,1... | collective-permute-start | bytes 1572872 | tf_op jit(solution)/shard_map/ppermute | solution.py:309
  68.7 31.5 %collective-permute-start.13 = (bf16[2,2,2,256,128]{4,3,2,1,0:T(8,128)(2,1)S(1)}, bf16[2,2,2,256,128]{4,3,2,1,0:T(8,128)(2,1)S(1)}, u32[]{:S(2)}, u32[]{:S(2)}) collective-permute-start(bf16[2,2,2,256,128]{4,3,2,1,0:T(8,128)(2,1)S(1)} %pad_maximum_fusion.3.refs_7_), channel_id=1, source_target_pairs={{0,1},{1,2},{2,3},{3,4},{4,5},{5,6},{6,7},{7,8},{8,9},{9,10},{10,1... | collective-permute-start | bytes 1572872 | tf_op jit(solution)/shard_map/ppermute | solution.py:308
  70.6 35.1 %collective-permute-start.16 = (bf16[2,2,2,256,128]{4,3,2,1,0:T(8,128)(2,1)S(1)}, bf16[2,2,2,256,128]{4,3,2,1,0:T(8,128)(2,1)S(1)}, u32[]{:S(2)}, u32[]{:S(2)}) collective-permute-start(bf16[2,2,2,256,128]{4,3,2,1,0:T(8,128)(2,1)S(1)} %pad_maximum_fusion.2.refs_6_), channel_id=1, source_target_pairs={{1,0},{2,1},{3,2},{4,3},{5,4},{6,5},{7,6},{8,7},{9,8},{10,9},{11,1... | collective-permute-start | bytes 1572872 | tf_op jit(solution)/shard_map/ppermute | solution.py:309
  76.2 11.0 %collective-permute-start.23 = (bf16[2,256,128]{2,1,0:T(8,128)(2,1)S(1)}, bf16[2,256,128]{2,1,0:T(8,128)(2,1)S(1)}, u32[]{:S(2)}, u32[]{:S(2)}) collective-permute-start(bf16[2,256,128]{2,1,0:T(8,128)(2,1)S(1)} %pad_maximum_fusion.15), channel_id=1, source_target_pairs={{0,96},{32,128},{64,160},{96,192},{128,224},{160,0},{192,32},{224,... | collective-permute-start | bytes 393224 | tf_op jit(solution)/shard_map/ppermute | solution.py:289
  77.9 16.3 %collective-permute-start.24 = (bf16[2,256,128]{2,1,0:T(8,128)(2,1)S(1)}, bf16[2,256,128]{2,1,0:T(8,128)(2,1)S(1)}, u32[]{:S(2)}, u32[]{:S(2)}) collective-permute-start(bf16[2,256,128]{2,1,0:T(8,128)(2,1)S(1)} %pad_maximum_fusion.16), channel_id=1, source_target_pairs={{0,64},{32,96},{64,128},{96,160},{128,192},{160,224},{192,0},{224,... | collective-permute-start | bytes 393224 | tf_op jit(solution)/shard_map/ppermute | solution.py:289
  87.1 20.8 %collective-permute-start.11 = (bf16[2,2,2,256,128]{4,3,2,1,0:T(8,128)(2,1)S(1)}, bf16[2,2,2,256,128]{4,3,2,1,0:T(8,128)(2,1)S(1)}, u32[]{:S(2)}, u32[]{:S(2)}) collective-permute-start(bf16[2,2,2,256,128]{4,3,2,1,0:T(8,128)(2,1)S(1)} %pad_maximum_fusion.2.refs_6_), channel_id=1, source_target_pairs={{0,1},{1,2},{2,3},{3,4},{4,5},{5,6},{6,7},{7,8},{8,9},{9,10},{10,1... | collective-permute-start | bytes 1572872 | tf_op jit(solution)/shard_map/ppermute | solution.py:308
  94.3 13.8 %collective-permute-start.15 = (bf16[2,2,2,256,128]{4,3,2,1,0:T(8,128)(2,1)S(1)}, bf16[2,2,2,256,128]{4,3,2,1,0:T(8,128)(2,1)S(1)}, u32[]{:S(2)}, u32[]{:S(2)}) collective-permute-start(bf16[2,2,2,256,128]{4,3,2,1,0:T(8,128)(2,1)S(1)} %pad_maximum_fusion.1.refs_5_), channel_id=1, source_target_pairs={{1,0},{2,1},{3,2},{4,3},{5,4},{6,5},{7,6},{8,7},{9,8},{10,9},{11,1... | collective-permute-start | bytes 1572872 | tf_op jit(solution)/shard_map/ppermute | solution.py:309
  98.3 16.4 %collective-permute-start.8 = (bf16[2,2,2,256,128]{4,3,2,1,0:T(8,128)(2,1)S(1)}, bf16[2,2,2,256,128]{4,3,2,1,0:T(8,128)(2,1)S(1)}, u32[]{:S(2)}, u32[]{:S(2)}) collective-permute-start(bf16[2,2,2,256,128]{4,3,2,1,0:T(8,128)(2,1)S(1)} %pad_maximum_fusion.1.refs_5_), channel_id=1, source_target_pairs={{0,1},{1,2},{2,3},{3,4},{4,5},{5,6},{6,7},{7,8},{8,9},{9,10},{10,1... | collective-permute-start | bytes 1572872 | tf_op jit(solution)/shard_map/ppermute | solution.py:308
  100.2 18.7 %collective-permute-start.14 = (bf16[2,2,2,256,128]{4,3,2,1,0:T(8,128)(2,1)S(1)}, bf16[2,2,2,256,128]{4,3,2,1,0:T(8,128)(2,1)S(1)}, u32[]{:S(2)}, u32[]{:S(2)}) collective-permute-start(bf16[2,2,2,256,128]{4,3,2,1,0:T(8,128)(2,1)S(1)} %pad_maximum_fusion.refs_4_), channel_id=1, source_target_pairs={{1,0},{2,1},{3,2},{4,3},{5,4},{6,5},{7,6},{8,7},{9,8},{10,9},{11,1... | collective-permute-start | bytes 1572872 | tf_op jit(solution)/shard_map/ppermute | solution.py:309
  105.7 19.6 %collective-permute-start.5 = (bf16[2,2,2,256,128]{4,3,2,1,0:T(8,128)(2,1)S(1)}, bf16[2,2,2,256,128]{4,3,2,1,0:T(8,128)(2,1)S(1)}, u32[]{:S(2)}, u32[]{:S(2)}) collective-permute-start(bf16[2,2,2,256,128]{4,3,2,1,0:T(8,128)(2,1)S(1)} %pad_maximum_fusion.refs_4_), channel_id=1, source_target_pairs={{0,1},{1,2},{2,3},{3,4},{4,5},{5,6},{6,7},{7,8},{8,9},{9,10},{10,1... | collective-permute-start | bytes 1572872 | tf_op jit(solution)/shard_map/ppermute | solution.py:308
  107.9 33.3 %collective-permute-start.1 = (bf16[2,256,128]{2,1,0:T(8,128)(2,1)S(1)}, bf16[2,256,128]{2,1,0:T(8,128)(2,1)S(1)}, u32[]{:S(2)}, u32[]{:S(2)}) collective-permute-start(bf16[2,256,128]{2,1,0:T(8,128)(2,1)S(1)} %pad_maximum_fusion.12), channel_id=1, source_target_pairs={{0,192},{32,224},{64,0},{96,32},{128,64},{160,96},{192,128},{224,1... | collective-permute-start | bytes 393224 | tf_op jit(solution)/shard_map/ppermute | solution.py:289
  108.0 51.4 %collective-permute-start.19 = (bf16[2,256,128]{2,1,0:T(8,128)(2,1)S(1)}, bf16[2,256,128]{2,1,0:T(8,128)(2,1)S(1)}, u32[]{:S(2)}, u32[]{:S(2)}) collective-permute-start(bf16[2,256,128]{2,1,0:T(8,128)(2,1)S(1)} %pad_maximum_fusion.13), channel_id=1, source_target_pairs={{0,128},{32,160},{64,192},{96,224},{128,0},{160,32},{192,64},{224,... | collective-permute-start | bytes 393224 | tf_op jit(solution)/shard_map/ppermute | solution.py:289
  114.6 50.3 %collective-permute-start.20 = (bf16[2,256,128]{2,1,0:T(8,128)(2,1)S(1)}, bf16[2,256,128]{2,1,0:T(8,128)(2,1)S(1)}, u32[]{:S(2)}, u32[]{:S(2)}) collective-permute-start(bf16[2,256,128]{2,1,0:T(8,128)(2,1)S(1)} %pad_maximum_fusion.14), channel_id=1, source_target_pairs={{0,160},{32,192},{64,224},{96,0},{128,32},{160,64},{192,96},{224,1... | collective-permute-start | bytes 393224 | tf_op jit(solution)/shard_map/ppermute | solution.py:289
  118.9 80.8 %collective-permute-start.27 = (bf16[2,256,128]{2,1,0:T(8,128)(2,1)S(1)}, bf16[2,256,128]{2,1,0:T(8,128)(2,1)S(1)}, u32[]{:S(2)}, u32[]{:S(2)}) collective-permute-start(bf16[2,256,128]{2,1,0:T(8,128)(2,1)S(1)} %pad_maximum_fusion.17), channel_id=1, source_target_pairs={{0,32},{32,64},{64,96},{96,128},{128,160},{160,192},{192,224},{224... | collective-permute-start | bytes 393224 | tf_op jit(solution)/shard_map/ppermute | solution.py:289
  125.3 74.4 %collective-permute-start.28 = (bf16[2,256,128]{2,1,0:T(8,128)(2,1)S(1)}, bf16[2,256,128]{2,1,0:T(8,128)(2,1)S(1)}, u32[]{:S(2)}, u32[]{:S(2)}) collective-permute-start(bf16[2,256,128]{2,1,0:T(8,128)(2,1)S(1)} %pad_maximum_fusion.18), channel_id=1, source_target_pairs={{0,224},{32,0},{64,32},{96,64},{128,96},{160,128},{192,160},{224,1... | collective-permute-start | bytes 393224 | tf_op jit(solution)/shard_map/ppermute | solution.py:289
  141.2 51.4 %collective-permute-start.25 = (bf16[2,256,128]{2,1,0:T(8,128)(2,1)S(1)}, bf16[2,256,128]{2,1,0:T(8,128)(2,1)S(1)}, u32[]{:S(2)}, u32[]{:S(2)}) collective-permute-start(bf16[2,256,128]{2,1,0:T(8,128)(2,1)S(1)} %get-tuple-element.25), channel_id=1, source_target_pairs={{0,160},{32,192},{64,224},{96,0},{128,32},{160,64},{192,96},{224,1... | collective-permute-start | bytes 393224 | tf_op jit(solution)/shard_map/ppermute | solution.py:289
  159.5 14.3 %copy-start = (bf16[2,256,128]{2,1,0:T(8,128)(2,1)}, bf16[2,256,128]{2,1,0:T(8,128)(2,1)S(1)}, u32[]{:S(2)}) copy-start(bf16[2,256,128]{2,1,0:T(8,128)(2,1)S(1)} %get-tuple-element.21.refs_0_) | copy-start | bytes 393220
  159.5 33.2 %collective-permute-start.26 = (bf16[2,256,128]{2,1,0:T(8,128)(2,1)S(1)}, bf16[2,256,128]{2,1,0:T(8,128)(2,1)S(1)}, u32[]{:S(2)}, u32[]{:S(2)}) collective-permute-start(bf16[2,256,128]{2,1,0:T(8,128)(2,1)S(1)} %get-tuple-element.26), channel_id=1, source_target_pairs={{0,192},{32,224},{64,0},{96,32},{128,64},{160,96},{192,128},{224,1... | collective-permute-start | bytes 393224 | tf_op jit(solution)/shard_map/ppermute | solution.py:289
  164.9 8.8 %collective-permute-start.18 = (bf16[2,256,128]{2,1,0:T(8,128)(2,1)S(1)}, bf16[2,256,128]{2,1,0:T(8,128)(2,1)S(1)}, u32[]{:S(2)}, u32[]{:S(2)}) collective-permute-start(bf16[2,256,128]{2,1,0:T(8,128)(2,1)S(1)} %get-tuple-element.22), channel_id=1, source_target_pairs={{0,64},{32,96},{64,128},{96,160},{128,192},{160,224},{192,0},{224,... | collective-permute-start | bytes 393224 | tf_op jit(solution)/shard_map/ppermute | solution.py:289
  173.8 9.9 %copy-start.6 = (bf16[2,256,128]{2,1,0:T(8,128)(2,1)}, bf16[2,256,128]{2,1,0:T(8,128)(2,1)S(1)}, u32[]{:S(2)}) copy-start(bf16[2,256,128]{2,1,0:T(8,128)(2,1)S(1)} %collective-permute-done.18.refs_1_) | copy-start | bytes 393220
  173.8 9.4 %collective-permute-start.21 = (bf16[2,256,128]{2,1,0:T(8,128)(2,1)S(1)}, bf16[2,256,128]{2,1,0:T(8,128)(2,1)S(1)}, u32[]{:S(2)}, u32[]{:S(2)}) collective-permute-start(bf16[2,256,128]{2,1,0:T(8,128)(2,1)S(1)} %get-tuple-element.23), channel_id=1, source_target_pairs={{0,128},{32,160},{64,192},{96,224},{128,0},{160,32},{192,64},{224,... | collective-permute-start | bytes 393224 | tf_op jit(solution)/shard_map/ppermute | solution.py:289
  183.2 9.4 %copy-start.7 = (bf16[2,256,128]{2,1,0:T(8,128)(2,1)}, bf16[2,256,128]{2,1,0:T(8,128)(2,1)S(1)}, u32[]{:S(2)}) copy-start(bf16[2,256,128]{2,1,0:T(8,128)(2,1)S(1)} %collective-permute-done.21.refs_2_) | copy-start | bytes 393220
  183.2 9.4 %collective-permute-start.22 = (bf16[2,256,128]{2,1,0:T(8,128)(2,1)S(1)}, bf16[2,256,128]{2,1,0:T(8,128)(2,1)S(1)}, u32[]{:S(2)}, u32[]{:S(2)}) collective-permute-start(bf16[2,256,128]{2,1,0:T(8,128)(2,1)S(1)} %get-tuple-element.24), channel_id=1, source_target_pairs={{0,96},{32,128},{64,160},{96,192},{128,224},{160,0},{192,32},{224,... | collective-permute-start | bytes 393224 | tf_op jit(solution)/shard_map/ppermute | solution.py:289
  192.6 0.7 copy-start.8
  192.6 7.1 %copy-start.4 = (bf16[2,256,128]{2,1,0:T(8,128)(2,1)}, bf16[2,256,128]{2,1,0:T(8,128)(2,1)S(1)}, u32[]{:S(2)}) copy-start(bf16[2,256,128]{2,1,0:T(8,128)(2,1)S(1)} %collective-permute-done.25.refs_4_) | copy-start | bytes 393220
  192.7 20.4 %copy-start.5 = (bf16[2,256,128]{2,1,0:T(8,128)(2,1)}, bf16[2,256,128]{2,1,0:T(8,128)(2,1)S(1)}, u32[]{:S(2)}) copy-start(bf16[2,256,128]{2,1,0:T(8,128)(2,1)S(1)} %collective-permute-done.26.refs_5_) | copy-start | bytes 393220
  193.3 34.3 %collective-permute-start.31 = (bf16[6,256,128]{2,1,0:T(8,128)(2,1)S(1)}, bf16[6,256,128]{2,1,0:T(8,128)(2,1)S(1)}, u32[]{:S(2)}, u32[]{:S(2)}) collective-permute-start(bf16[6,256,128]{2,1,0:T(8,128)(2,1)S(1)} %slice_dynamic-update-slice_fusion), channel_id=1, source_target_pairs={{0,16},{16,0},{1,17},{17,1},{2,18},{18,2},{3,19},{19,3},{4,20},{20... | collective-permute-start | bytes 1179656 | tf_op jit(solution)/shard_map/ppermute | solution.py:285
  213.1 11.8 %collective-permute-start.29 = (bf16[2,256,128]{2,1,0:T(8,128)(2,1)S(1)}, bf16[2,256,128]{2,1,0:T(8,128)(2,1)S(1)}, u32[]{:S(2)}, u32[]{:S(2)}) collective-permute-start(bf16[2,256,128]{2,1,0:T(8,128)(2,1)S(1)} %get-tuple-element.27), channel_id=1, source_target_pairs={{0,224},{32,0},{64,32},{96,64},{128,96},{160,128},{192,160},{224,1... | collective-permute-start | bytes 393224 | tf_op jit(solution)/shard_map/ppermute | solution.py:289
  218.8 6.1 %collective-permute-start.30 = (bf16[2,256,128]{2,1,0:T(8,128)(2,1)S(1)}, bf16[2,256,128]{2,1,0:T(8,128)(2,1)S(1)}, u32[]{:S(2)}, u32[]{:S(2)}) collective-permute-start(bf16[2,256,128]{2,1,0:T(8,128)(2,1)S(1)} %get-tuple-element.28), channel_id=1, source_target_pairs={{0,32},{32,64},{64,96},{96,128},{128,160},{160,192},{192,224},{224... | collective-permute-start | bytes 393224 | tf_op jit(solution)/shard_map/ppermute | solution.py:289
  224.9 0.7 copy-start.10
  225.6 2.0 collective-permute-start.32
  227.6 0.7 copy-start.11
  228.2 0.8 copy-start.3
  (3 other events, 2.0 us)

commit v2 on v1

--- a/solution.py
+++ b/solution.py
@@ -20,7 +20,7 @@
 SUB = 256
 GROUPS = ((0, 2), (4, 3), (5, 6), (7, 1))
 ARRIVAL = (1, 7, 2, 6, 3, 5, 4)
-PIECES = ((1, 7), (2, 6), (3, 5), (0, 4))
+PIECES = ((1, 2, 6, 7), (0, 3, 4, 5))
 BF16 = jnp.bfloat16
 HBM = pl.BlockSpec(memory_space=pltpu.HBM)
 VMEM = pl.BlockSpec(memory_space=pltpu.VMEM)
@@ -112,7 +112,7 @@
 
 
 def attend_body(sc, q0, q1, qse, *refs):
-    kv, (o0, o1), scratch = refs[:12], refs[12:14], refs[14:]
+    kv, (o0, o1), scratch = refs[:6], refs[6:8], refs[8:]
     buf, sem, flag, qbuf, acc, s0, s1, p0, p1 = scratch
     zpos, core = sc[0], sc[1]
     scores, probs = (s0, s1), (p0, p1)
@@ -124,12 +124,14 @@
     def start(t, carry):
         pack = t // 8
         rel = lax.rem(t - pack * 8 - zpos + 8, 8)
-        piece = lax.rem(jnp.minimum(rel, 8 - rel) + 3, 4)
-        for n in range(12):
-
-            @pl.when(pack * 4 + piece == n)
+        away = jnp.minimum(rel, 8 - rel)
+        near = jnp.where((away == 1) | (away == 2), 0, 1)
+        spot = jnp.where(near == 0, jnp.where(rel < 4, rel - 1, rel - 4), jnp.where(rel == 0, 0, rel - 2))
+        for n in range(6):
+
+            @pl.when(pack * 2 + near == n)
             def _():
-                pltpu.make_async_copy(kv[n].at[rel // 4], buf.at[t], sem.at[t]).start()
+                pltpu.make_async_copy(kv[n].at[spot], buf.at[t], sem.at[t]).start()
 
         flag[t] = 0
         return carry
@@ -240,7 +242,7 @@
     return pl.pallas_call(
         attend_body,
         out_shape=(block, block),
-        in_specs=[SMEM, VMEM, VMEM, VMEM] + [HBM] * 12,
+        in_specs=[SMEM, VMEM, VMEM, VMEM] + [HBM] * 6,
         out_specs=(VMEM, VMEM),
         scratch_shapes=[
             pltpu.VMEM((24, 2, 2, SUB, 128), BF16),
@@ -302,7 +304,7 @@
 def with_neighbours(arrived):
     forward = [(i, i + 1) for i in range(15)]
     backward = [(i + 1, i) for i in range(15)]
-    pieces = [jnp.stack([arrived[a], arrived[b]]) for a, b in PIECES]
+    pieces = [jnp.stack([arrived[r] for r in rels]) for rels in PIECES]
     before, after = [], []
     for piece in pieces:
         before.append(lax.ppermute(piece, "dp", forward))

time: 235 us -> 228 us (0.970)
  starting transfers between devices: 103 us -> 79.6 us
  waiting for transfers between devices: 54.1 us -> 71.6 us
    ppermute x4 -> x2, starting transfers between devices: 19.5 us -> 9.23 us  [with_neighbours(): after.append(lax.ppermute(piece, 'dp', backward))]
    ppermute x21, waiting for transfers between devices: 50.6 us -> 60.9 us  [z_shift(): return lax.ppermute(x, 'z', [(i, (i + k) % 8) for i in range(8)])]
    ppermute x21, starting transfers between devices: 66.1 us -> 58.9 us  [z_shift(): return lax.ppermute(x, 'z', [(i, (i + k) % 8) for i in range(8)])]
    ppermute x4 -> x2, waiting for transfers between devices: 1.34 us -> 6.37 us  [with_neighbours(): before.append(lax.ppermute(piece, 'dp', forward))]
    ppermute x4 -> x2, starting transfers between devices: 8.81 us -> 5.11 us  [with_neighbours(): before.append(lax.ppermute(piece, 'dp', forward))]
  transfers between devices with their start and end apart: 33 -> 29, of which waited for: 10 -> 13; matrix products, arithmetic and copies ran while one was open for 1% -> 1% of each run, Pallas kernels for 24% -> 24%
where the time goes in v2:
time: 228 us; the launch traced here: 225 us
  starting transfers between devices  79.6 us (35%)
  waiting for transfers between devices  71.6 us (31%)
  Pallas kernels  62.8 us (28%)
  local copies, waits for them, and re-layouts  5.81 us (3%)
  other arithmetic  4.16 us (2%)
    ppermute x21, waiting for transfers between devices, z_shift(): return lax.ppermute(x, 'z', [(i, (i + k) % 8) for i in range(8)])  60.9 us
    ppermute x21, starting transfers between devices, z_shift(): return lax.ppermute(x, 'z', [(i, (i + k) % 8) for i in range(8)])  58.9 us
    pallas_call x4, Pallas kernels, attend(): pl.pallas_call(attend_body, out_shape=(block, block), in_specs=[SMEM, VME...  48.3 us
    pallas_call x2, Pallas kernels, head_blocks(): pl.pallas_call(body, out_shape=(out, out), in_specs=[SMEM] + [VMEM] * (le...  11.8 us
    ppermute x2, starting transfers between devices, with_neighbours(): after.append(lax.ppermute(piece, 'dp', backward))  9.23 us
    ppermute x4, starting transfers between devices, core_swap(): return lax.ppermute(x, 'c', [(0, 1), (1, 0)])  6.38 us
    ppermute x2, waiting for transfers between devices, with_neighbours(): before.append(lax.ppermute(piece, 'dp', forward))  6.37 us
    ppermute x2, starting transfers between devices, with_neighbours(): before.append(lax.ppermute(piece, 'dp', forward))  5.11 us
  transfers between devices with their start and end apart: 29, of which 13 were waited for; matrix products, arithmetic and copies ran while one was open for 1% of the time, Pallas kernels for 24%

profile of v2, /device:TPU:5, one launch (start us, length us, event | category | flops | bytes accessed | tf_op | source)
XLA Modules:
  0.0 224.5 jit_solution(505137605320340182)
XLA Ops:
  0.0 0.7 copy-done.12
  0.7 0.7 copy-done.13
  1.7 0.6 pad_add_fusion.2
  2.7 0.6 copy-done.14
  3.3 1.3 fusion
  4.6 5.3 %shard_map.109 = (bf16[8,256,128]{2,1,0:T(8,128)(2,1)}, bf16[8,256,128]{2,1,0:T(8,128)(2,1)}) custom-call(s32[2]{0:T(128)} %get-tuple-element.90.pos, bf16[256,2048]{1,0:T(8,128)(2,1)} %bitcast.47, f32[1,128]{1,0:T(1,128)} %bitcast.50, f32[256,128]{1,0:T(8,128)} %get-tuple-element.77.cos, f32[256,128]{1,0:T(8,128)} %get-tuple-element.76.sin), custom_call_target="tpu_custom_call" | custom-call | flops 2000000000 | bytes 4000000 | tf_op jit(solution)/shard_map/pallas_call | solution.py:103
  9.9 0.7 collective-permute-start
  10.6 6.4 %shard_map.110 = (bf16[8,2,256,128]{3,2,1,0:T(8,128)(2,1)}, bf16[8,2,256,128]{3,2,1,0:T(8,128)(2,1)}) custom-call(s32[2]{0:T(128)} %get-tuple-element.90.pos, bf16[256,2048]{1,0:T(8,128)(2,1)} %bitcast.48, bf16[256,2048]{1,0:T(8,128)(2,1)} %bitcast.49, f32[1,128]{1,0:T(1,128)} %bitcast.51, f32[256,128]{1,0:T(8,128)} %get-tuple-element.77.cos, ...), custom_call_target="tpu_custom_call" | custom-call | flops 2000000000 | bytes 4000000 | tf_op jit(solution)/shard_map/pallas_call | solution.py:103
  19.1 0.8 collective-permute-done.2
  20.0 5.7 %collective-permute-start.3 = (bf16[2,2,256,128]{3,2,1,0:T(8,128)(2,1)S(1)}, bf16[2,2,256,128]{3,2,1,0:T(8,128)(2,1)S(1)}, u32[]{:S(2)}, u32[]{:S(2)}) collective-permute-start(bf16[2,2,256,128]{3,2,1,0:T(8,128)(2,1)S(1)} %pad_maximum_fusion.2), channel_id=1, source_target_pairs={{0,224},{32,0},{64,32},{96,64},{128,96},{160,128},{192,160},{224,1... | collective-permute-start | bytes 786440 | tf_op jit(solution)/shard_map/ppermute | solution.py:291
  25.7 1.7 collective-permute-start.8
  27.6 3.1 %collective-permute-start.10 = (bf16[2,2,256,128]{3,2,1,0:T(8,128)(2,1)S(1)}, bf16[2,2,256,128]{3,2,1,0:T(8,128)(2,1)S(1)}, u32[]{:S(2)}, u32[]{:S(2)}) collective-permute-start(bf16[2,2,256,128]{3,2,1,0:T(8,128)(2,1)S(1)} %pad_maximum_fusion.8), channel_id=1, source_target_pairs={{0,96},{32,128},{64,160},{96,192},{128,224},{160,0},{192,32},{224,... | collective-permute-start | bytes 786440 | tf_op jit(solution)/shard_map/ppermute | solution.py:291
  30.7 28.6 %collective-permute-done.8 = bf16[2,2,256,128]{3,2,1,0:T(8,128)(2,1)S(1)} collective-permute-done((bf16[2,2,256,128]{3,2,1,0:T(8,128)(2,1)S(1)}, bf16[2,2,256,128]{3,2,1,0:T(8,128)(2,1)S(1)}, u32[]{:S(2)}, u32[]{:S(2)}) %collective-permute-start.8) | collective-permute-done | bytes 262176 | tf_op jit(solution)/shard_map/ppermute | solution.py:291
  59.3 2.4 %collective-permute-start.5 = (bf16[2,2,256,128]{3,2,1,0:T(8,128)(2,1)S(1)}, bf16[2,2,256,128]{3,2,1,0:T(8,128)(2,1)S(1)}, u32[]{:S(2)}, u32[]{:S(2)}) collective-permute-start(bf16[2,2,256,128]{3,2,1,0:T(8,128)(2,1)S(1)} %pad_maximum_fusion.4), channel_id=1, source_target_pairs={{0,64},{32,96},{64,128},{96,160},{128,192},{160,224},{192,0},{224,... | collective-permute-start | bytes 786440 | tf_op jit(solution)/shard_map/ppermute | solution.py:291
  61.7 3.0 %collective-permute-start.6 = (bf16[2,2,256,128]{3,2,1,0:T(8,128)(2,1)S(1)}, bf16[2,2,256,128]{3,2,1,0:T(8,128)(2,1)S(1)}, u32[]{:S(2)}, u32[]{:S(2)}) collective-permute-start(bf16[2,2,256,128]{3,2,1,0:T(8,128)(2,1)S(1)} %pad_maximum_fusion.5), channel_id=1, source_target_pairs={{0,32},{32,64},{64,96},{96,128},{128,160},{160,192},{192,224},{224... | collective-permute-start | bytes 786440 | tf_op jit(solution)/shard_map/ppermute | solution.py:291
  64.9 4.6 %collective-permute-start.13 = (bf16[4,2,2,256,128]{4,3,2,1,0:T(8,128)(2,1)S(1)}, bf16[4,2,2,256,128]{4,3,2,1,0:T(8,128)(2,1)S(1)}, u32[]{:S(2)}, u32[]{:S(2)}) collective-permute-start(bf16[4,2,2,256,128]{4,3,2,1,0:T(8,128)(2,1)S(1)} %pad_maximum_fusion.1.refs_3_), channel_id=1, source_target_pairs={{1,0},{2,1},{3,2},{4,3},{5,4},{6,5},{7,6},{8,7},{9,8},{10,9},{11,1... | collective-permute-start | bytes 3145736 | tf_op jit(solution)/shard_map/ppermute | solution.py:311
  69.8 3.2 %collective-permute-start.11 = (bf16[4,2,2,256,128]{4,3,2,1,0:T(8,128)(2,1)S(1)}, bf16[4,2,2,256,128]{4,3,2,1,0:T(8,128)(2,1)S(1)}, u32[]{:S(2)}, u32[]{:S(2)}) collective-permute-start(bf16[4,2,2,256,128]{4,3,2,1,0:T(8,128)(2,1)S(1)} %pad_maximum_fusion.1.refs_3_), channel_id=1, source_target_pairs={{0,1},{1,2},{2,3},{3,4},{4,5},{5,6},{6,7},{7,8},{8,9},{9,10},{10,1... | collective-permute-start | bytes 3145736 | tf_op jit(solution)/shard_map/ppermute | solution.py:310
  73.0 4.8 %collective-permute-done.6 = bf16[2,2,256,128]{3,2,1,0:T(8,128)(2,1)S(1)} collective-permute-done((bf16[2,2,256,128]{3,2,1,0:T(8,128)(2,1)S(1)}, bf16[2,2,256,128]{3,2,1,0:T(8,128)(2,1)S(1)}, u32[]{:S(2)}, u32[]{:S(2)}) %collective-permute-start.6) | collective-permute-done | bytes 262176 | tf_op jit(solution)/shard_map/ppermute | solution.py:291
  78.0 4.6 %collective-permute-start.12 = (bf16[4,2,2,256,128]{4,3,2,1,0:T(8,128)(2,1)S(1)}, bf16[4,2,2,256,128]{4,3,2,1,0:T(8,128)(2,1)S(1)}, u32[]{:S(2)}, u32[]{:S(2)}) collective-permute-start(bf16[4,2,2,256,128]{4,3,2,1,0:T(8,128)(2,1)S(1)} %pad_maximum_fusion.refs_2_), channel_id=1, source_target_pairs={{1,0},{2,1},{3,2},{4,3},{5,4},{6,5},{7,6},{8,7},{9,8},{10,9},{11,1... | collective-permute-start | bytes 3145736 | tf_op jit(solution)/shard_map/ppermute | solution.py:311
  82.6 1.9 collective-permute-start.7
  84.6 0.9 collective-permute-start.19
  85.5 8.8 %collective-permute-done.19.q0 = bf16[2,256,128]{2,1,0:T(8,128)(2,1)S(1)} collective-permute-done((bf16[2,256,128]{2,1,0:T(8,128)(2,1)S(1)}, bf16[2,256,128]{2,1,0:T(8,128)(2,1)S(1)}, u32[]{:S(2)}, u32[]{:S(2)}) %collective-permute-start.19) | collective-permute-done | bytes 131104 | tf_op jit(solution)/shard_map/ppermute | solution.py:291
  94.4 5.8 %collective-permute-start.20 = (bf16[2,256,128]{2,1,0:T(8,128)(2,1)S(1)}, bf16[2,256,128]{2,1,0:T(8,128)(2,1)S(1)}, u32[]{:S(2)}, u32[]{:S(2)}) collective-permute-start(bf16[2,256,128]{2,1,0:T(8,128)(2,1)S(1)} %pad_maximum_fusion.14), channel_id=1, source_target_pairs={{0,64},{32,96},{64,128},{96,160},{128,192},{160,224},{192,0},{224,... | collective-permute-start | bytes 393224 | tf_op jit(solution)/shard_map/ppermute | solution.py:291
  100.2 2.9 %collective-permute-done.20.q1 = bf16[2,256,128]{2,1,0:T(8,128)(2,1)S(1)} collective-permute-done((bf16[2,256,128]{2,1,0:T(8,128)(2,1)S(1)}, bf16[2,256,128]{2,1,0:T(8,128)(2,1)S(1)}, u32[]{:S(2)}, u32[]{:S(2)}) %collective-permute-start.20) | collective-permute-done | bytes 131104 | tf_op jit(solution)/shard_map/ppermute | solution.py:291
  103.3 5.2 %collective-permute-start.15 = (bf16[2,256,128]{2,1,0:T(8,128)(2,1)S(1)}, bf16[2,256,128]{2,1,0:T(8,128)(2,1)S(1)}, u32[]{:S(2)}, u32[]{:S(2)}) collective-permute-start(bf16[2,256,128]{2,1,0:T(8,128)(2,1)S(1)} %pad_maximum_fusion.11), channel_id=1, source_target_pairs={{0,128},{32,160},{64,192},{96,224},{128,0},{160,32},{192,64},{224,... | collective-permute-start | bytes 393224 | tf_op jit(solution)/shard_map/ppermute | solution.py:291
  108.5 2.5 %collective-permute-done.12.refs_4_ = bf16[4,2,2,256,128]{4,3,2,1,0:T(8,128)(2,1)S(1)} collective-permute-done((bf16[4,2,2,256,128]{4,3,2,1,0:T(8,128)(2,1)S(1)}, bf16[4,2,2,256,128]{4,3,2,1,0:T(8,128)(2,1)S(1)}, u32[]{:S(2)}, u32[]{:S(2)}) %collective-permute-start.12) | collective-permute-done | bytes 1048608 | tf_op jit(solution)/shard_map/ppermute | solution.py:311
  111.1 6.4 %collective-permute-done.7.refs_0_ = bf16[4,2,2,256,128]{4,3,2,1,0:T(8,128)(2,1)S(1)} collective-permute-done((bf16[4,2,2,256,128]{4,3,2,1,0:T(8,128)(2,1)S(1)}, bf16[4,2,2,256,128]{4,3,2,1,0:T(8,128)(2,1)S(1)}, u32[]{:S(2)}, u32[]{:S(2)}) %collective-permute-start.7) | collective-permute-done | bytes 1048608 | tf_op jit(solution)/shard_map/ppermute | solution.py:310
  117.4 5.7 %collective-permute-start.24 = (bf16[2,256,128]{2,1,0:T(8,128)(2,1)S(1)}, bf16[2,256,128]{2,1,0:T(8,128)(2,1)S(1)}, u32[]{:S(2)}, u32[]{:S(2)}) collective-permute-start(bf16[2,256,128]{2,1,0:T(8,128)(2,1)S(1)} %pad_maximum_fusion.16), channel_id=1, source_target_pairs={{0,224},{32,0},{64,32},{96,64},{128,96},{160,128},{192,160},{224,1... | collective-permute-start | bytes 393224 | tf_op jit(solution)/shard_map/ppermute | solution.py:291
  123.1 12.3 %shard_map.113 = (bf16[2,256,128]{2,1,0:T(8,128)(2,1)S(1)}, bf16[2,256,128]{2,1,0:T(8,128)(2,1)S(1)}) custom-call(s32[10]{0:T(128)S(1)} %get-tuple-element.87.sc, bf16[2,256,128]{2,1,0:T(8,128)(2,1)S(1)} %collective-permute-done.19.q0, bf16[2,256,128]{2,1,0:T(8,128)(2,1)S(1)} %collective-permute-done.20.q1, s32[2,2,512]{2,1,0:T(2,128)S(1)} %get-tuple-element.75.qse, ...), custom_call_target="tpu_custom_call" | custom-call | flops 12000000000 | bytes 8000000 | tf_op jit(solution)/shard_map/pallas_call | solution.py:242
  135.4 4.2 %collective-permute-start.21 = (bf16[2,256,128]{2,1,0:T(8,128)(2,1)S(1)}, bf16[2,256,128]{2,1,0:T(8,128)(2,1)S(1)}, u32[]{:S(2)}, u32[]{:S(2)}) collective-permute-start(bf16[2,256,128]{2,1,0:T(8,128)(2,1)S(1)} %get-tuple-element.25), channel_id=1, source_target_pairs={{0,160},{32,192},{64,224},{96,0},{128,32},{160,64},{192,96},{224,1... | collective-permute-start | bytes 393224 | tf_op jit(solution)/shard_map/ppermute | solution.py:291
  139.6 14.8 %shard_map.111 = (bf16[2,256,128]{2,1,0:T(8,128)(2,1)S(1)}, bf16[2,256,128]{2,1,0:T(8,128)(2,1)S(1)}) custom-call(s32[10]{0:T(128)S(1)} %get-tuple-element.89.sc, bf16[2,256,128]{2,1,0:T(8,128)(2,1)S(1)} %pad_maximum_fusion.9.q0, bf16[2,256,128]{2,1,0:T(8,128)(2,1)S(1)} %collective-permute-done.1.q1, s32[2,2,512]{2,1,0:T(2,128)S(1)} %get-tuple-element.73.qse, ...), custom_call_target="tpu_custom_call" | custom-call | flops 12000000000 | bytes 8000000 | tf_op jit(solution)/shard_map/pallas_call | solution.py:242
  154.4 4.3 %collective-permute-start.22 = (bf16[2,256,128]{2,1,0:T(8,128)(2,1)S(1)}, bf16[2,256,128]{2,1,0:T(8,128)(2,1)S(1)}, u32[]{:S(2)}, u32[]{:S(2)}) collective-permute-start(bf16[2,256,128]{2,1,0:T(8,128)(2,1)S(1)} %get-tuple-element.26), channel_id=1, source_target_pairs={{0,192},{32,224},{64,0},{96,32},{128,64},{160,96},{192,128},{224,1... | collective-permute-start | bytes 393224 | tf_op jit(solution)/shard_map/ppermute | solution.py:291
  158.7 8.6 %shard_map.112 = (bf16[2,256,128]{2,1,0:T(8,128)(2,1)S(1)}, bf16[2,256,128]{2,1,0:T(8,128)(2,1)S(1)}) custom-call(s32[10]{0:T(128)S(1)} %get-tuple-element.88.sc, bf16[2,256,128]{2,1,0:T(8,128)(2,1)S(1)} %collective-permute-done.15.q0, bf16[2,256,128]{2,1,0:T(8,128)(2,1)S(1)} %collective-permute-done.16.q1, s32[2,2,512]{2,1,0:T(2,128)S(1)} %get-tuple-element.74.qse, ...), custom_call_target="tpu_custom_call" | custom-call | flops 12000000000 | bytes 8000000 | tf_op jit(solution)/shard_map/pallas_call | solution.py:242
  167.4 6.5 %collective-permute-start.17 = (bf16[2,256,128]{2,1,0:T(8,128)(2,1)S(1)}, bf16[2,256,128]{2,1,0:T(8,128)(2,1)S(1)}, u32[]{:S(2)}, u32[]{:S(2)}) collective-permute-start(bf16[2,256,128]{2,1,0:T(8,128)(2,1)S(1)} %get-tuple-element.23), channel_id=1, source_target_pairs={{0,128},{32,160},{64,192},{96,224},{128,0},{160,32},{192,64},{224,... | collective-permute-start | bytes 393224 | tf_op jit(solution)/shard_map/ppermute | solution.py:291
  173.9 2.3 %collective-permute-done.17.refs_2_ = bf16[2,256,128]{2,1,0:T(8,128)(2,1)S(1)} collective-permute-done((bf16[2,256,128]{2,1,0:T(8,128)(2,1)S(1)}, bf16[2,256,128]{2,1,0:T(8,128)(2,1)S(1)}, u32[]{:S(2)}, u32[]{:S(2)}) %collective-permute-start.17) | collective-permute-done | bytes 131104 | tf_op jit(solution)/shard_map/ppermute | solution.py:291
  176.6 9.3 %collective-permute-done.18.refs_3_ = bf16[2,256,128]{2,1,0:T(8,128)(2,1)S(1)} collective-permute-done((bf16[2,256,128]{2,1,0:T(8,128)(2,1)S(1)}, bf16[2,256,128]{2,1,0:T(8,128)(2,1)S(1)}, u32[]{:S(2)}, u32[]{:S(2)}) %collective-permute-start.18) | collective-permute-done | bytes 131104 | tf_op jit(solution)/shard_map/ppermute | solution.py:291
  186.0 0.5 copy-done.8
  186.6 4.5 %collective-permute-start.27 = (bf16[6,256,128]{2,1,0:T(8,128)(2,1)S(1)}, bf16[6,256,128]{2,1,0:T(8,128)(2,1)S(1)}, u32[]{:S(2)}, u32[]{:S(2)}) collective-permute-start(bf16[6,256,128]{2,1,0:T(8,128)(2,1)S(1)} %slice_dynamic-update-slice_fusion), channel_id=1, source_target_pairs={{0,16},{16,0},{1,17},{17,1},{2,18},{18,2},{3,19},{19,3},{4,20},{20... | collective-permute-start | bytes 1179656 | tf_op jit(solution)/shard_map/ppermute | solution.py:287
  191.1 12.6 %shard_map.114 = (bf16[2,256,128]{2,1,0:T(8,128)(2,1)S(1)}, bf16[2,256,128]{2,1,0:T(8,128)(2,1)S(1)}) custom-call(s32[10]{0:T(128)S(1)} %get-tuple-element.38.sc, bf16[2,256,128]{2,1,0:T(8,128)(2,1)S(1)} %collective-permute-done.23.q0, bf16[2,256,128]{2,1,0:T(8,128)(2,1)S(1)} %collective-permute-done.24.q1, s32[2,2,512]{2,1,0:T(2,128)S(1)} %get-tuple-element.72.qse, ...), custom_call_target="tpu_custom_call" | custom-call | flops 12000000000 | bytes 8000000 | tf_op jit(solution)/shard_map/pallas_call | solution.py:242
  203.7 7.9 %collective-permute-start.25 = (bf16[2,256,128]{2,1,0:T(8,128)(2,1)S(1)}, bf16[2,256,128]{2,1,0:T(8,128)(2,1)S(1)}, u32[]{:S(2)}, u32[]{:S(2)}) collective-permute-start(bf16[2,256,128]{2,1,0:T(8,128)(2,1)S(1)} %get-tuple-element.27), channel_id=1, source_target_pairs={{0,224},{32,0},{64,32},{96,64},{128,96},{160,128},{192,160},{224,1... | collective-permute-start | bytes 393224 | tf_op jit(solution)/shard_map/ppermute | solution.py:291
  211.6 2.1 collective-permute-start.26
  213.7 3.7 %collective-permute-done.25.refs_6_ = bf16[2,256,128]{2,1,0:T(8,128)(2,1)S(1)} collective-permute-done((bf16[2,256,128]{2,1,0:T(8,128)(2,1)S(1)}, bf16[2,256,128]{2,1,0:T(8,128)(2,1)S(1)}, u32[]{:S(2)}, u32[]{:S(2)}) %collective-permute-start.25) | collective-permute-done | bytes 131104 | tf_op jit(solution)/shard_map/ppermute | solution.py:291
  217.6 0.5 copy-done.9
  218.2 1.2 collective-permute-start.28
  219.4 1.0 collective-permute-done.28.refs_9_
  220.4 0.7 copy-done.11
  221.1 0.7 copy-done.3
  221.8 2.7 %shard_map.115 = bf16[256,2048]{1,0:T(8,128)(2,1)} custom-call(s32[2]{0:T(128)} %get-tuple-element.90.pos, bf16[2,256,128]{2,1,0:T(8,128)(2,1)} %copy-done, bf16[2,256,128]{2,1,0:T(8,128)(2,1)} %copy-done.6, bf16[2,256,128]{2,1,0:T(8,128)(2,1)} %copy-done.7, bf16[2,256,128]{2,1,0:T(8,128)(2,1)} %copy-done.8, bf16[2,256,128]{2,1,0:T(8,128)(2,1)} %copy-done.4, ...), custom_call_target="tpu_custom_call" | custom-call | tf_op jit(solution)/shard_map/pallas_call | solution.py:278
  (118 shorter events, 4.6 us)
Async XLA Ops:
  0.0 0.7 copy-start.12
  0.7 0.7 copy-start.13
  2.6 0.7 copy-start.14
  2.7 0.7 copy-start.15
  2.7 0.7 copy-start.16
  9.9 74.6 %collective-permute-start = (bf16[8,256,128]{2,1,0:T(8,128)(2,1)}, bf16[8,256,128]{2,1,0:T(8,128)(2,1)S(1)}, u32[]{:S(2)}, u32[]{:S(2)}) collective-permute-start(bf16[8,256,128]{2,1,0:T(8,128)(2,1)} %get-tuple-element.18), channel_id=1, source_target_pairs={{0,16},{16,0},{1,17},{17,1},{2,18},{18,2},{3,19},{19,3},{4,20},{20... | collective-permute-start | bytes 1572872 | tf_op jit(solution)/shard_map/ppermute | solution.py:287
  10.6 6.4 %copy-start.17 = (s32[8]{0:T(128)S(1)}, s32[8]{0:T(128)}, u32[]{:S(2)}) copy-start(s32[8]{0:T(128)} %constant.81.clone) | copy-start | bytes 100
  10.6 8.4 %copy-start.2 = (bf16[8,256,128]{2,1,0:T(8,128)(2,1)S(1)}, bf16[8,256,128]{2,1,0:T(8,128)(2,1)}, u32[]{:S(2)}) copy-start(bf16[8,256,128]{2,1,0:T(8,128)(2,1)} %get-tuple-element.17) | copy-start | bytes 1572868
  17.0 2.0 copy-start.1
  17.0 2.9 %collective-permute-start.2 = (bf16[8,2,256,128]{3,2,1,0:T(8,128)(2,1)}, bf16[8,2,256,128]{3,2,1,0:T(8,128)(2,1)S(1)}, u32[]{:S(2)}, u32[]{:S(2)}) collective-permute-start(bf16[8,2,256,128]{3,2,1,0:T(8,128)(2,1)} %get-tuple-element.20), channel_id=1, source_target_pairs={{0,16},{16,0},{1,17},{17,1},{2,18},{18,2},{3,19},{19,3},{4,20},{20... | collective-permute-start | bytes 3145736 | tf_op jit(solution)/shard_map/ppermute | solution.py:287
  20.0 44.9 %collective-permute-start.3 = (bf16[2,2,256,128]{3,2,1,0:T(8,128)(2,1)S(1)}, bf16[2,2,256,128]{3,2,1,0:T(8,128)(2,1)S(1)}, u32[]{:S(2)}, u32[]{:S(2)}) collective-permute-start(bf16[2,2,256,128]{3,2,1,0:T(8,128)(2,1)S(1)} %pad_maximum_fusion.2), channel_id=1, source_target_pairs={{0,224},{32,0},{64,32},{96,64},{128,96},{160,128},{192,160},{224,1... | collective-permute-start | bytes 786440 | tf_op jit(solution)/shard_map/ppermute | solution.py:291
  25.7 33.6 %collective-permute-start.8 = (bf16[2,2,256,128]{3,2,1,0:T(8,128)(2,1)S(1)}, bf16[2,2,256,128]{3,2,1,0:T(8,128)(2,1)S(1)}, u32[]{:S(2)}, u32[]{:S(2)}) collective-permute-start(bf16[2,2,256,128]{3,2,1,0:T(8,128)(2,1)S(1)} %pad_maximum_fusion.6), channel_id=1, source_target_pairs={{0,160},{32,192},{64,224},{96,0},{128,32},{160,64},{192,96},{224,1... | collective-permute-start | bytes 786440 | tf_op jit(solution)/shard_map/ppermute | solution.py:291
  27.4 31.9 %collective-permute-start.9 = (bf16[2,2,256,128]{3,2,1,0:T(8,128)(2,1)S(1)}, bf16[2,2,256,128]{3,2,1,0:T(8,128)(2,1)S(1)}, u32[]{:S(2)}, u32[]{:S(2)}) collective-permute-start(bf16[2,2,256,128]{3,2,1,0:T(8,128)(2,1)S(1)} %pad_maximum_fusion.7), channel_id=1, source_target_pairs={{0,128},{32,160},{64,192},{96,224},{128,0},{160,32},{192,64},{224,... | collective-permute-start | bytes 786440 | tf_op jit(solution)/shard_map/ppermute | solution.py:291
  27.6 34.1 %collective-permute-start.10 = (bf16[2,2,256,128]{3,2,1,0:T(8,128)(2,1)S(1)}, bf16[2,2,256,128]{3,2,1,0:T(8,128)(2,1)S(1)}, u32[]{:S(2)}, u32[]{:S(2)}) collective-permute-start(bf16[2,2,256,128]{3,2,1,0:T(8,128)(2,1)S(1)} %pad_maximum_fusion.8), channel_id=1, source_target_pairs={{0,96},{32,128},{64,160},{96,192},{128,224},{160,0},{192,32},{224,... | collective-permute-start | bytes 786440 | tf_op jit(solution)/shard_map/ppermute | solution.py:291
  59.3 10.5 %collective-permute-start.4 = (bf16[2,2,256,128]{3,2,1,0:T(8,128)(2,1)S(1)}, bf16[2,2,256,128]{3,2,1,0:T(8,128)(2,1)S(1)}, u32[]{:S(2)}, u32[]{:S(2)}) collective-permute-start(bf16[2,2,256,128]{3,2,1,0:T(8,128)(2,1)S(1)} %pad_maximum_fusion.3), channel_id=1, source_target_pairs={{0,192},{32,224},{64,0},{96,32},{128,64},{160,96},{192,128},{224,1... | collective-permute-start | bytes 786440 | tf_op jit(solution)/shard_map/ppermute | solution.py:291
  59.3 13.7 %collective-permute-start.5 = (bf16[2,2,256,128]{3,2,1,0:T(8,128)(2,1)S(1)}, bf16[2,2,256,128]{3,2,1,0:T(8,128)(2,1)S(1)}, u32[]{:S(2)}, u32[]{:S(2)}) collective-permute-start(bf16[2,2,256,128]{3,2,1,0:T(8,128)(2,1)S(1)} %pad_maximum_fusion.4), channel_id=1, source_target_pairs={{0,64},{32,96},{64,128},{96,160},{128,192},{160,224},{192,0},{224,... | collective-permute-start | bytes 786440 | tf_op jit(solution)/shard_map/ppermute | solution.py:291
  61.7 16.2 %collective-permute-start.6 = (bf16[2,2,256,128]{3,2,1,0:T(8,128)(2,1)S(1)}, bf16[2,2,256,128]{3,2,1,0:T(8,128)(2,1)S(1)}, u32[]{:S(2)}, u32[]{:S(2)}) collective-permute-start(bf16[2,2,256,128]{3,2,1,0:T(8,128)(2,1)S(1)} %pad_maximum_fusion.5), channel_id=1, source_target_pairs={{0,32},{32,64},{64,96},{96,128},{128,160},{160,192},{192,224},{224... | collective-permute-start | bytes 786440 | tf_op jit(solution)/shard_map/ppermute | solution.py:291
  64.9 38.4 %collective-permute-start.13 = (bf16[4,2,2,256,128]{4,3,2,1,0:T(8,128)(2,1)S(1)}, bf16[4,2,2,256,128]{4,3,2,1,0:T(8,128)(2,1)S(1)}, u32[]{:S(2)}, u32[]{:S(2)}) collective-permute-start(bf16[4,2,2,256,128]{4,3,2,1,0:T(8,128)(2,1)S(1)} %pad_maximum_fusion.1.refs_3_), channel_id=1, source_target_pairs={{1,0},{2,1},{3,2},{4,3},{5,4},{6,5},{7,6},{8,7},{9,8},{10,9},{11,1... | collective-permute-start | bytes 3145736 | tf_op jit(solution)/shard_map/ppermute | solution.py:311
  69.8 38.8 %collective-permute-start.11 = (bf16[4,2,2,256,128]{4,3,2,1,0:T(8,128)(2,1)S(1)}, bf16[4,2,2,256,128]{4,3,2,1,0:T(8,128)(2,1)S(1)}, u32[]{:S(2)}, u32[]{:S(2)}) collective-permute-start(bf16[4,2,2,256,128]{4,3,2,1,0:T(8,128)(2,1)S(1)} %pad_maximum_fusion.1.refs_3_), channel_id=1, source_target_pairs={{0,1},{1,2},{2,3},{3,4},{4,5},{5,6},{6,7},{7,8},{8,9},{9,10},{10,1... | collective-permute-start | bytes 3145736 | tf_op jit(solution)/shard_map/ppermute | solution.py:310
  78.0 33.1 %collective-permute-start.12 = (bf16[4,2,2,256,128]{4,3,2,1,0:T(8,128)(2,1)S(1)}, bf16[4,2,2,256,128]{4,3,2,1,0:T(8,128)(2,1)S(1)}, u32[]{:S(2)}, u32[]{:S(2)}) collective-permute-start(bf16[4,2,2,256,128]{4,3,2,1,0:T(8,128)(2,1)S(1)} %pad_maximum_fusion.refs_2_), channel_id=1, source_target_pairs={{1,0},{2,1},{3,2},{4,3},{5,4},{6,5},{7,6},{8,7},{9,8},{10,9},{11,1... | collective-permute-start | bytes 3145736 | tf_op jit(solution)/shard_map/ppermute | solution.py:311
  82.6 34.9 %collective-permute-start.7 = (bf16[4,2,2,256,128]{4,3,2,1,0:T(8,128)(2,1)S(1)}, bf16[4,2,2,256,128]{4,3,2,1,0:T(8,128)(2,1)S(1)}, u32[]{:S(2)}, u32[]{:S(2)}) collective-permute-start(bf16[4,2,2,256,128]{4,3,2,1,0:T(8,128)(2,1)S(1)} %pad_maximum_fusion.refs_2_), channel_id=1, source_target_pairs={{0,1},{1,2},{2,3},{3,4},{4,5},{5,6},{6,7},{7,8},{8,9},{9,10},{10,1... | collective-permute-start | bytes 3145736 | tf_op jit(solution)/shard_map/ppermute | solution.py:310
  84.6 9.8 %collective-permute-start.19 = (bf16[2,256,128]{2,1,0:T(8,128)(2,1)S(1)}, bf16[2,256,128]{2,1,0:T(8,128)(2,1)S(1)}, u32[]{:S(2)}, u32[]{:S(2)}) collective-permute-start(bf16[2,256,128]{2,1,0:T(8,128)(2,1)S(1)} %pad_maximum_fusion.13), channel_id=1, source_target_pairs={{0,96},{32,128},{64,160},{96,192},{128,224},{160,0},{192,32},{224,... | collective-permute-start | bytes 393224 | tf_op jit(solution)/shard_map/ppermute | solution.py:291
  94.4 8.8 %collective-permute-start.20 = (bf16[2,256,128]{2,1,0:T(8,128)(2,1)S(1)}, bf16[2,256,128]{2,1,0:T(8,128)(2,1)S(1)}, u32[]{:S(2)}, u32[]{:S(2)}) collective-permute-start(bf16[2,256,128]{2,1,0:T(8,128)(2,1)S(1)} %pad_maximum_fusion.14), channel_id=1, source_target_pairs={{0,64},{32,96},{64,128},{96,160},{128,192},{160,224},{192,0},{224,... | collective-permute-start | bytes 393224 | tf_op jit(solution)/shard_map/ppermute | solution.py:291
  103.2 32.2 %collective-permute-start.1 = (bf16[2,256,128]{2,1,0:T(8,128)(2,1)S(1)}, bf16[2,256,128]{2,1,0:T(8,128)(2,1)S(1)}, u32[]{:S(2)}, u32[]{:S(2)}) collective-permute-start(bf16[2,256,128]{2,1,0:T(8,128)(2,1)S(1)} %pad_maximum_fusion.10), channel_id=1, source_target_pairs={{0,192},{32,224},{64,0},{96,32},{128,64},{160,96},{192,128},{224,1... | collective-permute-start | bytes 393224 | tf_op jit(solution)/shard_map/ppermute | solution.py:291
  103.3 51.1 %collective-permute-start.15 = (bf16[2,256,128]{2,1,0:T(8,128)(2,1)S(1)}, bf16[2,256,128]{2,1,0:T(8,128)(2,1)S(1)}, u32[]{:S(2)}, u32[]{:S(2)}) collective-permute-start(bf16[2,256,128]{2,1,0:T(8,128)(2,1)S(1)} %pad_maximum_fusion.11), channel_id=1, source_target_pairs={{0,128},{32,160},{64,192},{96,224},{128,0},{160,32},{192,64},{224,... | collective-permute-start | bytes 393224 | tf_op jit(solution)/shard_map/ppermute | solution.py:291
  108.5 50.2 %collective-permute-start.16 = (bf16[2,256,128]{2,1,0:T(8,128)(2,1)S(1)}, bf16[2,256,128]{2,1,0:T(8,128)(2,1)S(1)}, u32[]{:S(2)}, u32[]{:S(2)}) collective-permute-start(bf16[2,256,128]{2,1,0:T(8,128)(2,1)S(1)} %pad_maximum_fusion.12), channel_id=1, source_target_pairs={{0,160},{32,192},{64,224},{96,0},{128,32},{160,64},{192,96},{224,1... | collective-permute-start | bytes 393224 | tf_op jit(solution)/shard_map/ppermute | solution.py:291
  111.1 80.0 %collective-permute-start.23 = (bf16[2,256,128]{2,1,0:T(8,128)(2,1)S(1)}, bf16[2,256,128]{2,1,0:T(8,128)(2,1)S(1)}, u32[]{:S(2)}, u32[]{:S(2)}) collective-permute-start(bf16[2,256,128]{2,1,0:T(8,128)(2,1)S(1)} %pad_maximum_fusion.15), channel_id=1, source_target_pairs={{0,32},{32,64},{64,96},{96,128},{128,160},{160,192},{192,224},{224... | collective-permute-start | bytes 393224 | tf_op jit(solution)/shard_map/ppermute | solution.py:291
  117.4 73.7 %collective-permute-start.24 = (bf16[2,256,128]{2,1,0:T(8,128)(2,1)S(1)}, bf16[2,256,128]{2,1,0:T(8,128)(2,1)S(1)}, u32[]{:S(2)}, u32[]{:S(2)}) collective-permute-start(bf16[2,256,128]{2,1,0:T(8,128)(2,1)S(1)} %pad_maximum_fusion.16), channel_id=1, source_target_pairs={{0,224},{32,0},{64,32},{96,64},{128,96},{160,128},{192,160},{224,1... | collective-permute-start | bytes 393224 | tf_op jit(solution)/shard_map/ppermute | solution.py:291
  135.4 50.5 %collective-permute-start.21 = (bf16[2,256,128]{2,1,0:T(8,128)(2,1)S(1)}, bf16[2,256,128]{2,1,0:T(8,128)(2,1)S(1)}, u32[]{:S(2)}, u32[]{:S(2)}) collective-permute-start(bf16[2,256,128]{2,1,0:T(8,128)(2,1)S(1)} %get-tuple-element.25), channel_id=1, source_target_pairs={{0,160},{32,192},{64,224},{96,0},{128,32},{160,64},{192,96},{224,1... | collective-permute-start | bytes 393224 | tf_op jit(solution)/shard_map/ppermute | solution.py:291
  154.4 12.9 %copy-start = (bf16[2,256,128]{2,1,0:T(8,128)(2,1)}, bf16[2,256,128]{2,1,0:T(8,128)(2,1)S(1)}, u32[]{:S(2)}) copy-start(bf16[2,256,128]{2,1,0:T(8,128)(2,1)S(1)} %get-tuple-element.21.refs_0_) | copy-start | bytes 393220
  154.4 31.5 %collective-permute-start.22 = (bf16[2,256,128]{2,1,0:T(8,128)(2,1)S(1)}, bf16[2,256,128]{2,1,0:T(8,128)(2,1)S(1)}, u32[]{:S(2)}, u32[]{:S(2)}) collective-permute-start(bf16[2,256,128]{2,1,0:T(8,128)(2,1)S(1)} %get-tuple-element.26), channel_id=1, source_target_pairs={{0,192},{32,224},{64,0},{96,32},{128,64},{160,96},{192,128},{224,1... | collective-permute-start | bytes 393224 | tf_op jit(solution)/shard_map/ppermute | solution.py:291
  158.7 8.6 %collective-permute-start.14 = (bf16[2,256,128]{2,1,0:T(8,128)(2,1)S(1)}, bf16[2,256,128]{2,1,0:T(8,128)(2,1)S(1)}, u32[]{:S(2)}, u32[]{:S(2)}) collective-permute-start(bf16[2,256,128]{2,1,0:T(8,128)(2,1)S(1)} %get-tuple-element.22), channel_id=1, source_target_pairs={{0,64},{32,96},{64,128},{96,160},{128,192},{160,224},{192,0},{224,... | collective-permute-start | bytes 393224 | tf_op jit(solution)/shard_map/ppermute | solution.py:291
  167.4 9.2 %copy-start.6 = (bf16[2,256,128]{2,1,0:T(8,128)(2,1)}, bf16[2,256,128]{2,1,0:T(8,128)(2,1)S(1)}, u32[]{:S(2)}) copy-start(bf16[2,256,128]{2,1,0:T(8,128)(2,1)S(1)} %collective-permute-done.14.refs_1_) | copy-start | bytes 393220
  167.4 8.9 %collective-permute-start.17 = (bf16[2,256,128]{2,1,0:T(8,128)(2,1)S(1)}, bf16[2,256,128]{2,1,0:T(8,128)(2,1)S(1)}, u32[]{:S(2)}, u32[]{:S(2)}) collective-permute-start(bf16[2,256,128]{2,1,0:T(8,128)(2,1)S(1)} %get-tuple-element.23), channel_id=1, source_target_pairs={{0,128},{32,160},{64,192},{96,224},{128,0},{160,32},{192,64},{224,... | collective-permute-start | bytes 393224 | tf_op jit(solution)/shard_map/ppermute | solution.py:291
  176.2 9.7 %copy-start.7 = (bf16[2,256,128]{2,1,0:T(8,128)(2,1)}, bf16[2,256,128]{2,1,0:T(8,128)(2,1)S(1)}, u32[]{:S(2)}) copy-start(bf16[2,256,128]{2,1,0:T(8,128)(2,1)S(1)} %collective-permute-done.17.refs_2_) | copy-start | bytes 393220
  176.2 9.7 %collective-permute-start.18 = (bf16[2,256,128]{2,1,0:T(8,128)(2,1)S(1)}, bf16[2,256,128]{2,1,0:T(8,128)(2,1)S(1)}, u32[]{:S(2)}, u32[]{:S(2)}) collective-permute-start(bf16[2,256,128]{2,1,0:T(8,128)(2,1)S(1)} %get-tuple-element.24), channel_id=1, source_target_pairs={{0,96},{32,128},{64,160},{96,192},{128,224},{160,0},{192,32},{224,... | collective-permute-start | bytes 393224 | tf_op jit(solution)/shard_map/ppermute | solution.py:291
  185.9 0.7 copy-start.8
  185.9 5.2 %copy-start.4 = (bf16[2,256,128]{2,1,0:T(8,128)(2,1)}, bf16[2,256,128]{2,1,0:T(8,128)(2,1)S(1)}, u32[]{:S(2)}) copy-start(bf16[2,256,128]{2,1,0:T(8,128)(2,1)S(1)} %collective-permute-done.21.refs_4_) | copy-start | bytes 393220
  186.0 17.8 %copy-start.5 = (bf16[2,256,128]{2,1,0:T(8,128)(2,1)}, bf16[2,256,128]{2,1,0:T(8,128)(2,1)S(1)}, u32[]{:S(2)}) copy-start(bf16[2,256,128]{2,1,0:T(8,128)(2,1)S(1)} %collective-permute-done.22.refs_5_) | copy-start | bytes 393220
  186.6 33.9 %collective-permute-start.27 = (bf16[6,256,128]{2,1,0:T(8,128)(2,1)S(1)}, bf16[6,256,128]{2,1,0:T(8,128)(2,1)S(1)}, u32[]{:S(2)}, u32[]{:S(2)}) collective-permute-start(bf16[6,256,128]{2,1,0:T(8,128)(2,1)S(1)} %slice_dynamic-update-slice_fusion), channel_id=1, source_target_pairs={{0,16},{16,0},{1,17},{17,1},{2,18},{18,2},{3,19},{19,3},{4,20},{20... | collective-permute-start | bytes 1179656 | tf_op jit(solution)/shard_map/ppermute | solution.py:287
  203.7 13.7 %collective-permute-start.25 = (bf16[2,256,128]{2,1,0:T(8,128)(2,1)S(1)}, bf16[2,256,128]{2,1,0:T(8,128)(2,1)S(1)}, u32[]{:S(2)}, u32[]{:S(2)}) collective-permute-start(bf16[2,256,128]{2,1,0:T(8,128)(2,1)S(1)} %get-tuple-element.27), channel_id=1, source_target_pairs={{0,224},{32,0},{64,32},{96,64},{128,96},{160,128},{192,160},{224,1... | collective-permute-start | bytes 393224 | tf_op jit(solution)/shard_map/ppermute | solution.py:291
  211.6 5.9 %collective-permute-start.26 = (bf16[2,256,128]{2,1,0:T(8,128)(2,1)S(1)}, bf16[2,256,128]{2,1,0:T(8,128)(2,1)S(1)}, u32[]{:S(2)}, u32[]{:S(2)}) collective-permute-start(bf16[2,256,128]{2,1,0:T(8,128)(2,1)S(1)} %get-tuple-element.28), channel_id=1, source_target_pairs={{0,32},{32,64},{64,96},{96,128},{128,160},{160,192},{192,224},{224... | collective-permute-start | bytes 393224 | tf_op jit(solution)/shard_map/ppermute | solution.py:291
  217.5 0.6 copy-start.9
  217.6 0.7 copy-start.10
  218.2 2.2 collective-permute-start.28
  220.4 0.7 copy-start.11
  221.1 0.7 copy-start.3
